TPU v7x, 128 devices: a whole 4x4x4 slice. The times are simulated.
128 devices in a mesh: dp: 8 (over x, core), feat: 16 (over y, z).
Axes of the slice: x: 4, y: 4, z: 4, core: 2. Of those that a mesh axis runs over, the one named last changes fastest.
Arguments:
- features: bfloat16 [262144, 2048], P('dp', 'feat'), may hold values from -210 to 210
- labels: int32 [262144], P('dp'), may hold values from 0 to 63
- groups: int32 [262144], P('dp'), may hold values from 0 to 1023
- coefficients: float32 [2048, 64], P('feat'), may hold values from -0.125 to 0.125
- coef_momentum: float32 [2048, 64], P('feat'), may hold values from -6 to 6
- group_effects: float32 [1024, 64], P('feat'), may hold values from -4 to 4
- group_momentum: float32 [1024, 64], P('feat'), may hold values from -6 to 6
- log_scale: float32 [64], replicated, may hold values from -1.2 to 0.4
Outputs:
- new_coefficients: float32 [2048, 64], P('feat')
- new_coef_momentum: float32 [2048, 64], P('feat')
- new_group_effects: float32 [1024, 64], P('feat')
- new_group_momentum: float32 [1024, 64], P('feat')
- energy_change: float32 [], replicated
All inputs are finite; a program needn't handle non-finite values.
Results may differ from a plain program's by a relative error of at most 0.001.
The roundings to bfloat16 on the way count: a program that leaves them out, or rounds other values in their place, can miss the bound.
Values may be sent and summed in bfloat16 or wider, within the bound.
A program may use at most 128 MiB of HBM per device.

v0:
```python
import math

import jax
import jax.numpy as jnp
from jax import lax
from jax.sharding import Mesh
from jax.sharding import PartitionSpec as P

FEAT = ("feat_0", "feat_1")
DP = ("dp_0", "dp_1")
DP_FEAT = ("dp_0", "dp_1", "feat_0", "feat_1")


def joined_along(parts, dim):
    shape = list(parts.shape[1:])
    shape[dim] *= parts.shape[0]
    return jnp.moveaxis(parts, 0, dim).reshape(shape)


def one_gather(arrays, axis, dims):
    line = jnp.concatenate([a.reshape(-1) for a in arrays])
    lines, at, outs = (lax.all_gather(line, axis), 0, [])
    for a, dim in zip(arrays, dims):
        parts = lines[:, at : at + a.size].reshape(-1, *a.shape)
        outs.append(joined_along(parts, dim))
        at += a.size
    return tuple(outs)


def split_up(array, dim, devices):
    shape = array.shape
    parts = array.reshape(*shape[:dim], devices, shape[dim] // devices, *shape[dim + 1 :])
    return jnp.moveaxis(parts, dim, 0)


def sum_at_owner(array, axis, dim):
    parts = split_up(array, dim, lax.axis_size(axis))
    arrived = lax.all_to_all(parts, axis, split_axis=0, concat_axis=0, tiled=True)
    return arrived.sum(axis=0)


def sent_to_all(array, axis):
    devices = lax.axis_size(axis)
    return lax.all_to_all(
        jnp.broadcast_to(array[None], (devices, *array.shape)), axis, 0, 0, tiled=True
    )


def taken_together(array, axis):
    everything = sent_to_all(array, axis)
    return jnp.sum(everything, axis=0)


def together(arrays, axis):
    ends = [0]
    for a in arrays:
        ends.append(ends[-1] + a.size)
    so_far = taken_together(jnp.concatenate([a.ravel() for a in arrays]), axis)
    return tuple((so_far[b:e].reshape(a.shape) for a, b, e in zip(arrays, ends, ends[1:])))


def over_axes(array, axes):
    for axis in axes:
        array = lax.psum(array, axis)
    return array


def onehot_table(groups, width):
    ids = lax.broadcasted_iota(jnp.int32, (width, groups.shape[0]), 0)
    return (ids == groups[None, :]).astype(jnp.bfloat16)


def row_terms(logits, labels):
    largest = jnp.max(logits, axis=0, keepdims=True)
    shifted = logits - largest
    scaled = jnp.exp(shifted)
    normalizer = jnp.sum(scaled, axis=0, keepdims=True)
    probability = scaled / normalizer
    classes = lax.broadcasted_iota(jnp.int32, logits.shape, 0)
    target = (classes == labels[None, :]).astype(jnp.float32)
    loglik = jnp.sum(target * shifted, axis=0) - jnp.log(normalizer[0])
    residual = (target - probability).astype(jnp.bfloat16)
    return (loglik, residual)


def rows_evaluate(row_block, onehot, labels_mine, coef_now, group_now):
    whole_coef, whole_group = one_gather(
        (coef_now.astype(jnp.bfloat16), group_now.astype(jnp.bfloat16)), FEAT, (0, 0)
    )
    blocks = lax.axis_size(FEAT)
    width = row_block.shape[0]
    classes = whole_coef.shape[1]
    feat_block = whole_coef.shape[0] // blocks
    group_block = whole_group.shape[0] // blocks
    partial_value = jnp.einsum(
        "nfi,fik->fkn",
        row_block.reshape(width, blocks, feat_block),
        whole_coef.reshape(blocks, feat_block, classes),
        preferred_element_type=jnp.float32,
    )
    partial_value = partial_value + jnp.einsum(
        "fgn,fgk->fkn",
        onehot.reshape(blocks, group_block, width),
        whole_group.reshape(blocks, group_block, classes),
        preferred_element_type=jnp.float32,
    )
    logits = jnp.sum(partial_value, axis=0)
    loglik, residual = row_terms(logits, labels_mine)
    coef_grad = lax.dot_general(
        row_block, residual, (((0,), (1,)), ((), ())), preferred_element_type=jnp.float32
    )
    group_grad = lax.dot_general(
        onehot, residual, (((1,), (1,)), ((), ())), preferred_element_type=jnp.float32
    )
    coef_grad, group_grad = (sum_at_owner(coef_grad, FEAT, 0), sum_at_owner(group_grad, FEAT, 0))
    return (loglik, coef_grad, group_grad)


def reduce_data(coef_grad, group_grad):
    return together((coef_grad, group_grad), DP)


def per_device(
    features, labels, groups, coefficients, coef_momentum, group_effects, group_momentum, log_scale
):
    blocks = lax.axis_size(FEAT)
    slice_rows = labels.shape[0] // blocks
    offset = lax.axis_index(FEAT) * slice_rows
    labels_mine = lax.dynamic_slice_in_dim(labels, offset, slice_rows, 0)
    rows_total = labels.shape[0] * lax.axis_size(DP)
    group_total = group_effects.shape[0] * blocks
    step_coef = 4.0 / math.sqrt(rows_total)
    step_group = 4.0 * math.sqrt(group_total / rows_total)
    inv_var = jnp.exp(-2.0 * log_scale)
    row_block = lax.all_to_all(features, FEAT, split_axis=0, concat_axis=1, tiled=True)
    groups_mine = lax.dynamic_slice_in_dim(groups, offset, slice_rows, 0)
    onehot = onehot_table(groups_mine, group_total)

    def evaluate(coef_now, group_now):
        return rows_evaluate(row_block, onehot, labels_mine, coef_now, group_now)

    coef_old, coef_mom_old = (coefficients, coef_momentum)
    group_old, group_mom_old = (group_effects, group_momentum)
    weight = 1.0 / lax.axis_size(DP)
    loglik_old, coef_grad, group_grad = evaluate(coefficients, group_effects)
    coef_grad, group_grad = reduce_data(coef_grad, group_grad)
    coef_half = coef_mom_old + 0.5 * step_coef * (coef_grad - coef_old)
    group_half = group_mom_old + 0.5 * step_group * (group_grad - group_old * inv_var)
    coef_new = coef_old + step_coef * coef_half
    group_new = group_old + step_group * group_half
    coef_full, group_full = (coef_new, group_new)
    loglik_new, coef_grad, group_grad = evaluate(coef_full, group_full)
    coef_grad, group_grad = reduce_data(coef_grad, group_grad)
    coef_mom_new = coef_half + 0.5 * step_coef * (coef_grad - coef_new)
    group_mom_new = group_half + 0.5 * step_group * (group_grad - group_new * inv_var)
    state_terms = 0.5 * jnp.sum(coef_new * coef_new - coef_old * coef_old)
    state_terms = state_terms + 0.5 * jnp.sum(
        (group_new * group_new - group_old * group_old) * inv_var
    )
    state_terms = state_terms + 0.5 * jnp.sum(
        coef_mom_new * coef_mom_new - coef_mom_old * coef_mom_old
    )
    state_terms = state_terms + 0.5 * jnp.sum(
        group_mom_new * group_mom_new - group_mom_old * group_mom_old
    )
    local_terms = jnp.sum(loglik_old - loglik_new) + weight * state_terms
    energy = over_axes(local_terms.reshape(1), DP_FEAT)[0]
    coef_mom_full, group_mom_full = (coef_mom_new, group_mom_new)
    return (coef_full, coef_mom_full, group_full, group_mom_full, energy)


def solution(mesh):
    torus = Mesh(mesh.devices.reshape(4, 2, 4, 4), ("dp_0", "dp_1", "feat_0", "feat_1"))
    in_specs = (
        P(DP, FEAT),
        P(DP),
        P(DP),
        P(FEAT, None),
        P(FEAT, None),
        P(FEAT, None),
        P(FEAT, None),
        P(),
    )
    out_specs = (P(FEAT, None), P(FEAT, None), P(FEAT, None), P(FEAT, None), P())
    return jax.shard_map(
        per_device, mesh=torus, in_specs=in_specs, out_specs=out_specs, check_vma=False
    )
```

profile of v0, /device:TPU:1, one launch (start us, length us, event | category | flops | bytes accessed | tf_op | source)
XLA Modules:
  0.0 358.8 jit_solution(18150914982869518744)
XLA Ops:
  0.7 8.8 %all-to-all-start = ((bf16[16,2048,128]{2,1,0:T(8,128)(2,1)}), bf16[16,2048,128]{2,1,0:T(8,128)(2,1)}, u32[]{:S(2)}, u32[]{:S(2)}) async-start(bf16[16,2048,128]{2,1,0:T(8,128)(2,1)} %bitcast.47), calls=%async_computation | async-start | bytes 16777216 | tf_op jit(solution)/shard_map/all_to_all | solution.py:135
  9.8 159.0 %all-gather = bf16[196608]{0:T(1024)(128)(2,1)S(1)} all-gather(bf16[12288]{0:T(1024)(128)(2,1)S(1)} %pad_maximum_fusion.2), channel_id=2, replica_groups=mesh['dp_0'=4,'dp_1'=2,'feat_0'=4,'feat_1'=4] {'feat_0','feat_1'}, dimensions={0}, use_global_device_ids=true | all-gather | bytes 417792 | tf_op jit(solution)/shard_map/all_gather | solution.py:22
  169.0 0.7 dynamic_slice.6
  169.7 0.7 dynamic_slice.7
  170.7 0.5 reshape_reshape_reshape.12
  171.3 6.4 %fusion.20 = f32[16,64,2048]{2,1,0:T(8,128)S(1)} fusion(bf16[16,128,64]{2,1,0:T(8,128)(2,1)S(1)} %reshape_reshape_reshape.12, bf16[16,2048,128]{2,1,0:T(8,128)(2,1)} %all-to-all-done), kind=kOutput, calls=%fused_computation.47 | convolution fusion | flops 536870912 | bytes 17039360 | tf_op jit(solution)/shard_map/nfi,fik->fkn/dot_general | solution.py:95
  177.7 2.0 add_reduce_fusion.1
  180.1 1.7 fusion.5
  182.1 1.0 reshape.153
  183.2 5.7 %all-to-all-start.2 = ((f32[16,1,4096]{2,1,0:T(1,128)}), f32[16,1,4096]{2,1,0:T(1,128)S(1)}, u32[]{:S(2)}, u32[]{:S(2)}) async-start(f32[16,1,4096]{2,1,0:T(1,128)} %reshape.153), calls=%async_computation.2 | async-start | bytes 524288 | tf_op jit(solution)/shard_map/all_to_all | solution.py:38
  188.9 12.4 %copy.110 = bf16[2048,16,128]{0,2,1:T(8,128)(2,1)} copy(bf16[2048,16,128]{2,0,1:T(8,128)(2,1)} %bitcast.1) | data formatting | bytes 16777216 | tf_op jit(solution)/shard_map/all_to_all | solution.py:135
  201.3 6.0 %convolution_bitcast_fusion.1 = f32[8,16,8,128]{3,2,1,0:T(8,128)S(1)} fusion(bf16[64,2048]{1,0:T(8,128)(2,1)S(1)} %fusion.16, bf16[2048,2048]{0,1:T(8,128)(2,1)} %bitcast.45), kind=kOutput, calls=%fused_computation.16 | convolution fusion | flops 536870912 | bytes 9175040 | tf_op jit(solution)/shard_map/dot_general | solution.py:109
  207.3 0.8 copy.157
  208.2 6.7 %all-to-all-start.1 = ((f32[16,128,64]{1,2,0:T(8,128)}), f32[16,128,64]{1,2,0:T(8,128)S(1)}, u32[]{:S(2)}, u32[]{:S(2)}) async-start(f32[16,128,64]{1,2,0:T(8,128)} %bitcast.42), calls=%async_computation.1 | async-start | bytes 1048576 | tf_op jit(solution)/shard_map/all_to_all | solution.py:38
  214.9 0.5 broadcast.55
  215.4 1.3 reduce.2
  217.1 6.7 %all-to-all-done.1 = f32[16,128,64]{1,2,0:T(8,128)S(1)} async-done(((f32[16,128,64]{1,2,0:T(8,128)}), f32[16,128,64]{1,2,0:T(8,128)S(1)}, u32[]{:S(2)}, u32[]{:S(2)}) %all-to-all-start.1) | async-done | bytes 524320 | tf_op jit(solution)/shard_map/all_to_all | solution.py:38
  224.0 1.0 broadcast_in_dim.4
  225.0 13.1 %all-to-all-start.3 = ((f32[8,1,12288]{2,1,0:T(1,128)}), f32[8,1,12288]{2,1,0:T(1,128)S(1)}, u32[]{:S(2)}, u32[]{:S(2)}) async-start(f32[8,1,12288]{2,1,0:T(1,128)} %broadcast_in_dim.4), calls=%async_computation.3 | async-start | bytes 786432 | tf_op jit(solution)/shard_map/all_to_all | solution.py:44
  238.3 7.5 %all-to-all-done.3 = f32[8,1,12288]{2,1,0:T(1,128)S(1)} async-done(((f32[8,1,12288]{2,1,0:T(1,128)}), f32[8,1,12288]{2,1,0:T(1,128)S(1)}, u32[]{:S(2)}, u32[]{:S(2)}) %all-to-all-start.3) | async-done | bytes 393248 | tf_op jit(solution)/shard_map/all_to_all | solution.py:44
  245.8 0.3 reduce_sum.157
  246.3 0.6 multiply_reduce_fusion
  247.0 0.6 subtract_reduce_fusion.1
  247.7 16.8 %all-gather.1 = bf16[196608]{0:T(1024)(128)(2,1)S(1)} all-gather(bf16[12288]{0:T(1024)(128)(2,1)S(1)} %pad_maximum_fusion.3), channel_id=3, replica_groups=mesh['dp_0'=4,'dp_1'=2,'feat_0'=4,'feat_1'=4] {'feat_0','feat_1'}, dimensions={0}, use_global_device_ids=true | all-gather | bytes 417792 | tf_op jit(solution)/shard_map/all_gather | solution.py:22
  265.0 0.5 reshape_reshape_reshape.14
  265.5 6.4 %fusion.18 = f32[16,64,2048]{2,1,0:T(8,128)S(1)} fusion(bf16[16,128,64]{2,1,0:T(8,128)(2,1)S(1)} %reshape_reshape_reshape.14, bf16[16,2048,128]{2,1,0:T(8,128)(2,1)} %all-to-all-done), kind=kOutput, calls=%fused_computation.45 | convolution fusion | flops 536870912 | bytes 17039360 | tf_op jit(solution)/shard_map/nfi,fik->fkn/dot_general | solution.py:95
  272.0 2.0 add_reduce_fusion
  274.3 1.7 fusion.4
  276.4 1.0 reshape.155
  277.4 4.2 %all-to-all-start.5 = ((f32[16,1,4096]{2,1,0:T(1,128)}), f32[16,1,4096]{2,1,0:T(1,128)S(1)}, u32[]{:S(2)}, u32[]{:S(2)}) async-start(f32[16,1,4096]{2,1,0:T(1,128)} %reshape.155), calls=%async_computation.5 | async-start | bytes 524288 | tf_op jit(solution)/shard_map/all_to_all | solution.py:38
  281.7 6.0 %convolution_bitcast_fusion = f32[8,16,8,128]{3,2,1,0:T(8,128)S(1)} fusion(bf16[64,2048]{1,0:T(8,128)(2,1)S(1)} %fusion.17, bf16[2048,2048]{0,1:T(8,128)(2,1)} %bitcast.46), kind=kOutput, calls=%fused_computation.15 | convolution fusion | flops 536870912 | bytes 9175040 | tf_op jit(solution)/shard_map/dot_general | solution.py:109
  287.7 0.8 copy.156
  288.6 0.4 all-to-all-done.5
  289.0 6.2 %all-to-all-start.4 = ((f32[16,128,64]{1,2,0:T(8,128)}), f32[16,128,64]{1,2,0:T(8,128)S(1)}, u32[]{:S(2)}, u32[]{:S(2)}) async-start(f32[16,128,64]{1,2,0:T(8,128)} %bitcast.41), calls=%async_computation.4 | async-start | bytes 1048576 | tf_op jit(solution)/shard_map/all_to_all | solution.py:38
  295.2 1.3 reduce.3
  296.9 7.3 %all-to-all-done.4 = f32[16,128,64]{1,2,0:T(8,128)S(1)} async-done(((f32[16,128,64]{1,2,0:T(8,128)}), f32[16,128,64]{1,2,0:T(8,128)S(1)}, u32[]{:S(2)}, u32[]{:S(2)}) %all-to-all-start.4) | async-done | bytes 524320 | tf_op jit(solution)/shard_map/all_to_all | solution.py:38
  304.4 0.9 broadcast_in_dim.5
  305.3 11.8 %all-to-all-start.6 = ((f32[8,1,12288]{2,1,0:T(1,128)}), f32[8,1,12288]{2,1,0:T(1,128)S(1)}, u32[]{:S(2)}, u32[]{:S(2)}) async-start(f32[8,1,12288]{2,1,0:T(1,128)} %broadcast_in_dim.5), calls=%async_computation.6 | async-start | bytes 786432 | tf_op jit(solution)/shard_map/all_to_all | solution.py:44
  318.4 0.6 subtract_reduce_fusion.3
  319.0 5.8 %all-to-all-done.6 = f32[8,1,12288]{2,1,0:T(1,128)S(1)} async-done(((f32[8,1,12288]{2,1,0:T(1,128)}), f32[8,1,12288]{2,1,0:T(1,128)S(1)}, u32[]{:S(2)}, u32[]{:S(2)}) %all-to-all-start.6) | async-done | bytes 393248 | tf_op jit(solution)/shard_map/all_to_all | solution.py:44
  325.2 1.2 subtract_reduce_fusion.2
  326.5 0.6 subtract_reduce_fusion
  329.1 8.1 %psum.28 = f32[1]{0:T(128)} all-reduce(f32[1]{0:T(128)} %bitcast.5), channel_id=1, replica_groups=mesh['dp_0'=4,'dp_1'=2,'feat_0'=4,'feat_1'=4] {'dp_0'}, use_global_device_ids=true, to_apply=%region_19.0 | all-reduce | flops 1 | bytes 8 | tf_op jit(solution)/shard_map/psum | solution.py:64
  337.2 5.9 %psum.29 = f32[1]{0:T(128)} all-reduce(f32[1]{0:T(128)} %psum.28), channel_id=1, replica_groups=mesh['dp_0'=4,'dp_1'=2,'feat_0'=4,'feat_1'=4] {'dp_1'}, use_global_device_ids=true, to_apply=%region_20.0 | all-reduce | flops 1 | bytes 8 | tf_op jit(solution)/shard_map/psum | solution.py:64
  343.1 0.7 copy.134
  343.8 7.4 %psum.30 = f32[1]{0:T(128)} all-reduce(f32[1]{0:T(128)} %psum.29), channel_id=1, replica_groups=mesh['dp_0'=4,'dp_1'=2,'feat_0'=4,'feat_1'=4] {'feat_0'}, use_global_device_ids=true, to_apply=%region_21.0 | all-reduce | flops 1 | bytes 8 | tf_op jit(solution)/shard_map/psum | solution.py:64
  351.2 6.9 %psum.31 = f32[]{:T(128)} all-reduce(f32[]{:T(128)} %bitcast.6), channel_id=1, replica_groups=mesh['dp_0'=4,'dp_1'=2,'feat_0'=4,'feat_1'=4] {'feat_1'}, use_global_device_ids=true, to_apply=%region_22.0 | all-reduce | flops 1 | bytes 8 | tf_op jit(solution)/shard_map/psum | solution.py:64
  358.1 0.7 copy.135
  (72 shorter events, 4.7 us)
Async XLA Ops:
  0.6 8.8 %copy-start.2 = (f32[128,64]{0,1:T(8,128)S(1)}, f32[128,64]{0,1:T(8,128)}, u32[]{:S(2)}) copy-start(f32[128,64]{0,1:T(8,128)} %param.11) | copy-start | bytes 98308
  0.6 9.0 %copy-start = (f32[64,64]{1,0:T(8,128)S(1)}, f32[64,64]{1,0:T(8,128)}, u32[]{:S(2)}) copy-start(f32[64,64]{1,0:T(8,128)} %param.13) | copy-start | bytes 49156
  0.7 170.6 %all-to-all-start = ((bf16[16,2048,128]{2,1,0:T(8,128)(2,1)}), bf16[16,2048,128]{2,1,0:T(8,128)(2,1)}, u32[]{:S(2)}, u32[]{:S(2)}) async-start(bf16[16,2048,128]{2,1,0:T(8,128)(2,1)} %bitcast.47), calls=%async_computation | async-start | bytes 16777216 | tf_op jit(solution)/shard_map/all_to_all | solution.py:135
  183.2 25.0 %all-to-all-start.2 = ((f32[16,1,4096]{2,1,0:T(1,128)}), f32[16,1,4096]{2,1,0:T(1,128)S(1)}, u32[]{:S(2)}, u32[]{:S(2)}) async-start(f32[16,1,4096]{2,1,0:T(1,128)} %reshape.153), calls=%async_computation.2 | async-start | bytes 524288 | tf_op jit(solution)/shard_map/all_to_all | solution.py:38
  201.3 36.9 %copy-start.4 = (f32[128,64]{0,1:T(8,128)S(1)}, f32[128,64]{0,1:T(8,128)}, u32[]{:S(2)}) copy-start(f32[128,64]{0,1:T(8,128)} %param.12) | copy-start | bytes 98308
  201.3 37.0 %copy-start.5 = (f32[64]{0:T(128)S(1)}, f32[64]{0:T(128)}, u32[]{:S(2)}) copy-start(f32[64]{0:T(128)} %param.15) | copy-start | bytes 772
  201.3 45.0 %copy-start.3 = (f32[64,64]{1,0:T(8,128)S(1)}, f32[64,64]{1,0:T(8,128)}, u32[]{:S(2)}) copy-start(f32[64,64]{1,0:T(8,128)} %param.14) | copy-start | bytes 49156
  208.2 15.6 %all-to-all-start.1 = ((f32[16,128,64]{1,2,0:T(8,128)}), f32[16,128,64]{1,2,0:T(8,128)S(1)}, u32[]{:S(2)}, u32[]{:S(2)}) async-start(f32[16,128,64]{1,2,0:T(8,128)} %bitcast.42), calls=%async_computation.1 | async-start | bytes 1048576 | tf_op jit(solution)/shard_map/all_to_all | solution.py:38
  225.0 20.8 %all-to-all-start.3 = ((f32[8,1,12288]{2,1,0:T(1,128)}), f32[8,1,12288]{2,1,0:T(1,128)S(1)}, u32[]{:S(2)}, u32[]{:S(2)}) async-start(f32[8,1,12288]{2,1,0:T(1,128)} %broadcast_in_dim.4), calls=%async_computation.3 | async-start | bytes 786432 | tf_op jit(solution)/shard_map/all_to_all | solution.py:44
  246.9 78.3 %copy-start.1 = (f32[64,64]{1,0:T(8,128)}, f32[64,64]{1,0:T(8,128)S(1)}, u32[]{:S(2)}) copy-start(f32[64,64]{1,0:T(8,128)S(1)} %get-tuple-element.39) | copy-start | bytes 49156
  277.4 11.6 %all-to-all-start.5 = ((f32[16,1,4096]{2,1,0:T(1,128)}), f32[16,1,4096]{2,1,0:T(1,128)S(1)}, u32[]{:S(2)}, u32[]{:S(2)}) async-start(f32[16,1,4096]{2,1,0:T(1,128)} %reshape.155), calls=%async_computation.5 | async-start | bytes 524288 | tf_op jit(solution)/shard_map/all_to_all | solution.py:38
  289.0 15.2 %all-to-all-start.4 = ((f32[16,128,64]{1,2,0:T(8,128)}), f32[16,128,64]{1,2,0:T(8,128)S(1)}, u32[]{:S(2)}, u32[]{:S(2)}) async-start(f32[16,128,64]{1,2,0:T(8,128)} %bitcast.41), calls=%async_computation.4 | async-start | bytes 1048576 | tf_op jit(solution)/shard_map/all_to_all | solution.py:38
  305.3 19.5 %all-to-all-start.6 = ((f32[8,1,12288]{2,1,0:T(1,128)}), f32[8,1,12288]{2,1,0:T(1,128)S(1)}, u32[]{:S(2)}, u32[]{:S(2)}) async-start(f32[8,1,12288]{2,1,0:T(1,128)} %broadcast_in_dim.5), calls=%async_computation.6 | async-start | bytes 786432 | tf_op jit(solution)/shard_map/all_to_all | solution.py:44
where the time goes:
time: 363 us; the launch traced here: 359 us
  blocking collectives  204 us (56%)
  starting transfers between devices  56.5 us (16%)
  matrix products  32.4 us (9%)
  waiting for transfers between devices  27.7 us (8%)
  local copies, waits for them, and re-layouts  26 us (7%)
  other arithmetic  7.71 us (2%)
  between operations  4.31 us (1%)
    all_gather x2, blocking collectives, one_gather(): lines, at, outs = (lax.all_gather(line, axis), 0, [])  176 us
    psum x4, blocking collectives, over_axes(): array = lax.psum(array, axis)  28.3 us
    all_to_all x2, starting transfers between devices, sent_to_all(): lax.all_to_all(jnp.broadcast_to(array[None], (devices, *array.shape)), ax...  24.9 us
    all_to_all x4, starting transfers between devices, sum_at_owner(): lax.all_to_all(parts, axis, split_axis=0, concat_axis=0, tiled=True)  22.9 us
    all_to_all x4, waiting for transfers between devices, sum_at_owner(): lax.all_to_all(parts, axis, split_axis=0, concat_axis=0, tiled=True)  14.4 us
    all_to_all x2, waiting for transfers between devices, sent_to_all(): lax.all_to_all(jnp.broadcast_to(array[None], (devices, *array.shape)), ax...  13.3 us
    dot_general x2, matrix products, rows_evaluate(): jnp.einsum('nfi,fik->fkn', row_block.reshape(width, blocks, feat_block),...  12.9 us
    all_to_all x1, local copies, waits for them, and re-layouts, per_device(): lax.all_to_all(features, FEAT, split_axis=0, concat_axis=1, tiled=True)  12.4 us
  transfers between devices with their start and end apart: 7, of which 5 were waited for; matrix products, arithmetic and copies ran while one was open for 9% of the time, Pallas kernels for 0%

commit v1 on v0

v1 whole, which is shorter than its diff:
```python
import math

import jax
import jax.numpy as jnp
from jax import lax
from jax.experimental import pallas as pl
from jax.experimental.pallas import tpu as pltpu
from jax.sharding import Mesh
from jax.sharding import PartitionSpec as P

FEAT = ("feat_0", "feat_1")
DP = ("dp_0", "dp_1")

NC = 4
UNIT = 128
BF16, F32 = jnp.bfloat16, jnp.float32
NT = (((1,), (1,)), ((), ()))
NN = (((1,), (0,)), ((), ()))


def dot(a, b, dims):
    return lax.dot_general(a, b, dims, preferred_element_type=F32)


def kernel(rows_total, group_total, feats, labels, groups, pos_ref, mom_ref, iv_ref,
           new_ref, mom_out_ref, energy_ref,
           X, ST, OH, W, PL, R1, R2, RG, CS, CG, ACC, GS, GR, DS, DR, DG, EN, LL, HALF,
           loc_sem, a_s, a_r, rs_s, rs_r, g_s, g_r, c_s, c_r, q_s, q_r, d_s, d_r, b_s, b_r, e_s, e_r):
    x, core = lax.axis_index("dp_0"), lax.axis_index("dp_1")
    place = (lax.axis_index("feat_0"), lax.axis_index("feat_1"))
    dp = x * 2 + core
    classes = pos_ref.shape[0] - 32
    block_rows = NC * 8 * UNIT
    chunk_rows = 8 * UNIT

    def at(axis, step):
        return {FEAT[axis]: lax.rem(place[axis] + step, 4)}

    def dp_at(step):
        peer = lax.rem(dp + step, 8)
        return {"dp_0": peer // 2, "dp_1": lax.rem(peer, 2)}

    def remote(src, dst, s, r, device):
        return pltpu.make_async_remote_copy(
            src_ref=src, dst_ref=dst, send_sem=s, recv_sem=r,
            device_id=device, device_id_type=pl.DeviceIdType.MESH)

    def a2a(t, c, k):
        me = place[t]
        half = chunk_rows // 2

        def rows(step, part, count):
            first = (t * 4 + lax.rem(me + step, 4)) * block_rows + c * chunk_rows + part * half
            return feats.at[pl.ds(pl.multiple_of(first, half), count)]

        def to(r, part, count):
            return X.at[t, r, pl.ds(pl.multiple_of(c * chunk_rows + part * half, half), count)]

        sems = (a_s.at[t, c, k], a_r.at[t, c, k])
        if k == 0:
            return remote(rows(1, 0, chunk_rows), to(3, 0, chunk_rows), *sems, at(t, 1))
        if k == 1:
            return remote(rows(3, 0, chunk_rows), to(1, 0, chunk_rows), *sems, at(t, 3))
        if k == 2:
            return remote(rows(2, 0, half), ST.at[t, c, 0], *sems, at(t, 1))
        if k == 3:
            return remote(rows(2, 1, half), ST.at[t, c, 1], *sems, at(t, 3))
        if k == 4:
            return remote(ST.at[t, c, 0], to(2, 0, half), *sems, at(t, 1))
        return remote(ST.at[t, c, 1], to(2, 1, half), *sems, at(t, 3))

    def scatter(e, t, c, k):
        axis = 1 - t
        p = place[axis]
        step = 1 if k % 2 == 0 else 3
        owner = lax.rem(p + (2 if k < 2 else step), 4)
        h = (0, 1, 1, 0, 0, 1)[k]
        dst = R1.at[e, t, c, k] if k < 2 else R2.at[e, t, c, k % 2, h]
        return remote(PL.at[e, t, c, owner * 2 + h], dst, rs_s.at[e, t, c, k], rs_r.at[e, t, c, k], at(axis, step))

    def gather(e, t, c, k):
        axis = 1 - t
        p = place[axis]
        step = 1 if k % 2 == 0 else 3
        if k < 2:
            ref = RG.at[e, t, c, pl.ds(p * 2, 2)]
        else:
            ref = RG.at[e, t, c, lax.rem(p + 4 - step, 4) * 2 + (k - 2)]
        return remote(ref, ref, g_s.at[e, t, c, k], g_r.at[e, t, c, k], at(axis, step))

    def weights(e, t, r):
        return remote(CS.at[e], CG.at[e, t, 3 - r], c_s.at[e, t, r - 1], c_r.at[e, t, r - 1], at(t, r))

    def gradients(e, t, r):
        return remote(GS.at[e, t, r], GR.at[e, t, r - 1], q_s.at[e, t, r - 1], q_r.at[e, t, r - 1], at(t, r))

    def dp_scatter(e, k):
        return remote(DS.at[e, lax.rem(dp + k, 8)], DR.at[e, k - 1], d_s.at[e, k - 1], d_r.at[e, k - 1], dp_at(k))

    def dp_gather(e, k):
        return remote(DG.at[e, dp], DG.at[e, dp], b_s.at[e, k - 1], b_r.at[e, k - 1], dp_at(k))

    def energies(k):
        mine = place[0] * 4 + place[1]
        device = {**at(0, k // 4), **at(1, k % 4)}
        return remote(EN.at[mine], EN.at[mine], e_s.at[k - 1], e_r.at[k - 1], device)

    barrier = pltpu.get_barrier_semaphore()
    for k in range(1, 16):
        pl.semaphore_signal(barrier, inc=1, device_id={**at(0, k // 4), **at(1, k % 4)},
                            device_id_type=pl.DeviceIdType.MESH)
    for k in range(1, 8):
        pl.semaphore_signal(barrier, inc=1, device_id=dp_at(k), device_id_type=pl.DeviceIdType.MESH)

    def own(t):
        first = (t * 4 + place[t]) * block_rows
        return pltpu.make_async_copy(feats.at[pl.ds(pl.multiple_of(first, block_rows), block_rows)], X.at[t, 0],
                                     loc_sem.at[t])

    own(0).start()
    own(1).start()
    CS[0] = pos_ref[...].astype(BF16)
    pl.semaphore_wait(barrier, 22)

    lane = lax.broadcasted_iota(jnp.int32, (32, 128), 1)
    low = lane < 64

    def send_weights(e):
        for t in range(2):
            for r in (1, 3, 2):
                weights(e, t, r).start()

    def gather_weights(e):
        for t in range(2):
            for r in (1, 3, 2):
                weights(e, t, r).wait_recv()
            packed = []
            for r in range(4):
                block = CS[e] if r == 0 else CG[e, t, r - 1]
                W[t, :, r * 128:(r + 1) * 128] = block[:classes]
                packed.append(block[classes:].astype(F32))
            for i in range(2):
                a, b = packed[2 * i], packed[2 * i + 1]
                lanes = pl.ds(512 + i * 128, 128)
                W[t, 0:32, lanes] = jnp.where(low, a, pltpu.roll(b, 64, 1)).astype(BF16)
                W[t, 32:64, lanes] = jnp.where(low, pltpu.roll(a, 64, 1), b).astype(BF16)

    def send_features(c):
        for k in (2, 3, 0, 1):
            for t in range(2):
                a2a(t, c, k).start()

    def pass_features(c):
        for k in (2, 3):
            for t in range(2):
                a2a(t, c, k).wait_recv()
                a2a(t, c, k + 2).start()

    def wait_features(c):
        for k in (0, 1, 4, 5):
            for t in range(2):
                a2a(t, c, k).wait_recv()

    def pair(t, r, rows):
        return jnp.concatenate([X[t, r, rows, :], X[t, r + 1, rows, :]], axis=1)

    def rows_of(c, o):
        return pl.ds(pl.multiple_of(c * chunk_rows + o * 256, 256), 256)

    def logits(e, c):
        for t in range(2):
            def block(o, _):
                rows = rows_of(c, o)
                total = dot(W[t, :, 0:256], pair(t, 0, rows), NT)
                total = total + dot(W[t, :, 256:512], pair(t, 2, rows), NT)
                total = total + dot(W[t, :, 512:768], OH[t, c * 4 + o], NN)
                PL[e, t, c, o * 2] = total[:, :128]
                PL[e, t, c, o * 2 + 1] = total[:, 128:]
                return 0
            lax.fori_loop(0, 4, block, 0)
            for k in range(4):
                scatter(e, t, c, k).start()

    def add_passed(e, c):
        for t in range(2):
            p = place[1 - t]
            for k in range(2):
                scatter(e, t, c, k).wait_recv()
                unit = lax.rem(p + (1 if k == 0 else 3), 4) * 2 + k
                PL[e, t, c, unit] = PL[e, t, c, unit] + R1[e, t, c, k]
            for k in (4, 5):
                scatter(e, t, c, k).start()

    def softmax(e, c):
        for t in range(2):
            p = place[1 - t]
            for k in range(2, 6):
                scatter(e, t, c, k).wait_recv()
            for h in range(2):
                value = PL[e, t, c, p * 2 + h] + R2[e, t, c, 0, h] + R2[e, t, c, 1, h]
                unit = ((t * 4 + place[t]) * NC + c) * 8 + p * 2 + h
                label = labels[pl.ds(unit, 1), :]
                shifted = value - jnp.max(value, axis=0, keepdims=True)
                scaled = jnp.exp(shifted)
                normalizer = jnp.sum(scaled, axis=0, keepdims=True)
                hit = lax.broadcasted_iota(jnp.int32, value.shape, 0) == label
                loglik = jnp.sum(jnp.where(hit, shifted, 0.0), axis=0, keepdims=True) - jnp.log(normalizer)
                LL[e, t, c, h] = jnp.broadcast_to(loglik, (8, 128))
                probability = scaled * (1.0 / normalizer)
                RG[e, t, c, p * 2 + h] = (jnp.where(hit, 1.0, 0.0) - probability).astype(BF16)
            for k in range(2):
                gather(e, t, c, k).start()

    def pass_residual(e, c):
        for t in range(2):
            for k in range(2):
                gather(e, t, c, k).wait_recv()
                gather(e, t, c, k + 2).start()

    def gradient(e, c):
        for t in range(2):
            for k in (2, 3):
                gather(e, t, c, k).wait_recv()

            def block(o, _):
                rows = rows_of(c, o)
                res = jnp.concatenate([RG[e, t, c, o * 2], RG[e, t, c, o * 2 + 1]], axis=1)
                ACC[t, :, 0:256] += dot(res, pair(t, 0, rows), NN)
                ACC[t, :, 256:512] += dot(res, pair(t, 2, rows), NN)
                ACC[t, :, 512:768] += dot(res, OH[t, c * 4 + o], NT)
                return 0
            lax.fori_loop(0, 4, block, 0)

    def reduce_gradient(e):
        for t in range(2):
            for r in (1, 3, 2, 0):
                GS[e, t, r, 0:classes] = ACC[t, :, r * 128:(r + 1) * 128]
                tile = 512 + (r // 2) * 128
                top, bottom = ACC[t, 0:32, tile:tile + 128], ACC[t, 32:64, tile:tile + 128]
                if r % 2 == 0:
                    GS[e, t, r, classes:] = jnp.where(low, top, pltpu.roll(bottom, 64, 1))
                else:
                    GS[e, t, r, classes:] = jnp.where(low, pltpu.roll(top, 64, 1), bottom)
                if r:
                    gradients(e, t, r).start()
        total = GS[e, 0, 0] + GS[e, 1, 0]
        for r in (1, 3, 2):
            for t in range(2):
                gradients(e, t, r).wait_recv()
                total = total + GR[e, t, r - 1]
        for i in range(6):
            DS[e, i] = total[i * 16:(i + 1) * 16]
        for k in range(1, 8):
            dp_scatter(e, k).start()
        mine = DS[e, dp]
        for k in range(1, 8):
            dp_scatter(e, k).wait_recv()
            mine = mine + DR[e, k - 1]
        DG[e, dp, 0:16] = mine
        for k in range(1, 8):
            dp_gather(e, k).start()
        for k in range(1, 8):
            dp_gather(e, k).wait_recv()
        return jnp.concatenate([DG[e, i, 0:16] for i in range(6)], axis=0)

    send_weights(0)
    send_features(0)

    for e in range(2):
        for i in (6, 7):
            DS[e, i] = jnp.zeros((16, 128), F32)
    DG[0, dp, 16:24] = jnp.zeros((8, 128), F32)

    ids = lax.broadcasted_iota(jnp.int32, (64, 128), 0)
    for t in range(2):
        def onehot(b, _):
            for h in range(2):
                unit = (t * 4 + place[t]) * (NC * 8) + b * 2 + h
                group = groups[pl.ds(unit, 1), :]
                for r in range(4):
                    other = lax.rem(place[t] + r, 4)
                    owner = other * 4 + place[1] if t == 0 else place[0] * 4 + other
                    hit = ids + owner * 64 == group
                    OH[t, b, r * 64:(r + 1) * 64, h * 128:(h + 1) * 128] = jnp.where(hit, 1.0, 0.0).astype(BF16)
            return 0
        lax.fori_loop(0, NC * 4, onehot, 0)
    gather_weights(0)
    ACC[...] = jnp.zeros_like(ACC)
    own(0).wait()
    own(1).wait()

    def slot(s, _):
        def stage(lag, body):
            c = s - lag
            pl.when(jnp.logical_and(c >= 0, c < NC))(lambda: body(c))
        stage(-1, send_features)
        stage(0, pass_features)

        def first(c):
            wait_features(c)
            logits(0, c)
        stage(1, first)
        stage(2, lambda c: add_passed(0, c))
        stage(3, lambda c: softmax(0, c))
        stage(4, lambda c: pass_residual(0, c))
        stage(5, lambda c: gradient(0, c))
        return 0
    lax.fori_loop(0, NC + 5, slot, 0)

    grad = reduce_gradient(0)
    row = lax.broadcasted_iota(jnp.int32, grad.shape, 0)
    step = jnp.where(row < classes, 4.0 / math.sqrt(rows_total), 4.0 * math.sqrt(group_total / rows_total))
    half = mom_ref[...] + 0.5 * step * (grad - pos_ref[...] * iv_ref[...])
    new = pos_ref[...] + step * half
    CS[1] = new.astype(BF16)
    send_weights(1)
    new_ref[...] = new
    HALF[...] = half

    ACC[...] = jnp.zeros_like(ACC)
    gather_weights(1)
    for body in (logits, add_passed, softmax, pass_residual, gradient):
        def over(c, _, body=body):
            body(1, c)
            return 0
        lax.fori_loop(0, NC, over, 0)

    change = jnp.zeros((8, 128), F32)
    for t in range(2):
        for c in range(NC):
            for h in range(2):
                change = change + (LL[0, t, c, h] - LL[1, t, c, h])
    DG[1, dp, 16:24] = change
    grad = reduce_gradient(1)
    half, new = HALF[...], new_ref[...]
    mom = half + 0.5 * step * (grad - new * iv_ref[...])
    mom_out_ref[...] = mom
    state = 0.5 * ((new * new - pos_ref[...] * pos_ref[...]) * iv_ref[...] + (mom * mom - mom_ref[...] * mom_ref[...]))
    terms = jnp.broadcast_to(jnp.sum(state, axis=0, keepdims=True), (8, 128))
    for i in range(8):
        terms = terms + DG[1, i, 16:24]
    EN[place[0] * 4 + place[1]] = terms
    for k in range(1, 16):
        energies(k).start()
    for k in range(1, 16):
        energies(k).wait_recv()
    terms = EN[0]
    for i in range(1, 16):
        terms = terms + EN[i]
    energy_ref[...] = jnp.broadcast_to(jnp.sum(terms, axis=1, keepdims=True), (8, 128))

    def sent(c, _):
        for t in range(2):
            for k in range(6):
                a2a(t, c, k).wait_send()
                for e in range(2):
                    scatter(e, t, c, k).wait_send()
                    if k < 4:
                        gather(e, t, c, k).wait_send()
        return 0
    lax.fori_loop(0, NC, sent, 0)
    for e in range(2):
        for t in range(2):
            for r in range(1, 4):
                weights(e, t, r).wait_send()
                gradients(e, t, r).wait_send()
        for k in range(1, 8):
            dp_scatter(e, k).wait_send()
            dp_gather(e, k).wait_send()
    for k in range(1, 16):
        energies(k).wait_send()


def packed(coef, group):
    turned = group.T
    return jnp.concatenate([coef.T, jnp.concatenate([turned[:32], turned[32:]], axis=1)], axis=0)


def unpacked(both, classes):
    tail = both[classes:]
    return both[:classes].T, jnp.concatenate([tail[:, :64], tail[:, 64:]], axis=0).T


def per_device(
    features, labels, groups, coefficients, coef_momentum, group_effects, group_momentum, log_scale
):
    rows = labels.shape[0]
    classes = coefficients.shape[1]
    rows_total = rows * lax.axis_size(DP)
    group_total = group_effects.shape[0] * lax.axis_size(FEAT)
    pos = packed(coefficients, group_effects)
    mom = packed(coef_momentum, group_momentum)
    inv_var = jnp.broadcast_to(jnp.exp(-2.0 * log_scale)[None, :], (64, classes))
    iv = packed(jnp.ones_like(coefficients), inv_var)
    vmem = pl.BlockSpec(memory_space=pltpu.VMEM)
    dma = pltpu.SemaphoreType.DMA
    new, new_mom, energy = pl.pallas_call(
        lambda *refs: kernel(rows_total, group_total, *refs),
        out_shape=[jax.ShapeDtypeStruct((96, 128), F32), jax.ShapeDtypeStruct((96, 128), F32),
                   jax.ShapeDtypeStruct((8, 128), F32)],
        in_specs=[pl.BlockSpec(memory_space=pl.ANY)] + [vmem] * 5,
        out_specs=[vmem] * 3,
        scratch_shapes=[
            pltpu.VMEM((2, 4, NC * 1024, 128), BF16),
            pltpu.VMEM((2, NC, 2, 512, 128), BF16),
            pltpu.VMEM((2, NC * 4, 256, 256), BF16),
            pltpu.VMEM((2, 64, 768), BF16),
            pltpu.VMEM((2, 2, NC, 8, 64, 128), F32),
            pltpu.VMEM((2, 2, NC, 2, 64, 128), F32),
            pltpu.VMEM((2, 2, NC, 2, 2, 64, 128), F32),
            pltpu.VMEM((2, 2, NC, 8, 64, 128), BF16),
            pltpu.VMEM((2, 96, 128), BF16),
            pltpu.VMEM((2, 2, 3, 96, 128), BF16),
            pltpu.VMEM((2, 64, 768), F32),
            pltpu.VMEM((2, 2, 4, 96, 128), F32),
            pltpu.VMEM((2, 2, 3, 96, 128), F32),
            pltpu.VMEM((2, 8, 16, 128), F32),
            pltpu.VMEM((2, 7, 16, 128), F32),
            pltpu.VMEM((2, 8, 24, 128), F32),
            pltpu.VMEM((16, 8, 128), F32),
            pltpu.VMEM((2, 2, NC, 2, 8, 128), F32),
            pltpu.VMEM((96, 128), F32),
            dma((2,)),
            dma((2, NC, 6)), dma((2, NC, 6)),
            dma((2, 2, NC, 6)), dma((2, 2, NC, 6)),
            dma((2, 2, NC, 4)), dma((2, 2, NC, 4)),
            dma((2, 2, 3)), dma((2, 2, 3)),
            dma((2, 2, 3)), dma((2, 2, 3)),
            dma((2, 7)), dma((2, 7)),
            dma((2, 7)), dma((2, 7)),
            dma((15,)), dma((15,)),
        ],
        compiler_params=pltpu.CompilerParams(
            collective_id=0, has_side_effects=True, vmem_limit_bytes=56 * 2**20),
        name="leapfrog",
    )(features, labels.reshape(-1, 128), groups.reshape(-1, 128), pos, mom, iv)
    new_coef, new_group = unpacked(new, classes)
    new_coef_mom, new_group_mom = unpacked(new_mom, classes)
    return (new_coef, new_coef_mom, new_group, new_group_mom, energy[0, 0])


def solution(mesh):
    torus = Mesh(mesh.devices.reshape(4, 2, 4, 4), ("dp_0", "dp_1", "feat_0", "feat_1"))
    in_specs = (
        P(DP, FEAT),
        P(DP),
        P(DP),
        P(FEAT, None),
        P(FEAT, None),
        P(FEAT, None),
        P(FEAT, None),
        P(),
    )
    out_specs = (P(FEAT, None), P(FEAT, None), P(FEAT, None), P(FEAT, None), P())
    return jax.shard_map(
        per_device, mesh=torus, in_specs=in_specs, out_specs=out_specs, check_vma=False
    )
```

time: 363 us -> 155 us (0.43)
  blocking collectives: 204 us -> 0 us
  Pallas kernels: 0 us -> 143 us
  starting transfers between devices: 56.5 us -> 0 us
  matrix products: 32.4 us -> 0 us
  waiting for transfers between devices: 27.7 us -> 0 us
  local copies, waits for them, and re-layouts: 26 us -> 6.75 us
  between operations: 4.31 us -> 0.66 us
    all_gather x2 -> x0, blocking collectives: 176 us -> none  [one_gather(): lines, at, outs = (lax.all_gather(line, axis), 0, [])]
    pallas_call x0 -> x1, Pallas kernels: none -> 143 us  [per_device(): pl.pallas_call(lambda *refs: kernel(rows_total, group_total, *refs), out_...]
    all_to_all x7 -> x0, starting transfers between devices: 56.5 us -> none  [the longest x2 24.9 us: sent_to_all(): lax.all_to_all(jnp.broadcast_to(array[None], (devices, *array.shape)), ax...]
    dot_general x8 -> x0, matrix products: 32.4 us -> none  [the longest x2 12.9 us: rows_evaluate(): jnp.einsum('nfi,fik->fkn', row_block.reshape(width, blocks, feat_block),...]
    psum x4 -> x0, blocking collectives: 28.3 us -> none  [over_axes(): array = lax.psum(array, axis)]
    all_to_all x7 -> x0, waiting for transfers between devices: 27.7 us -> none  [the longest x4 14.4 us: sum_at_owner(): lax.all_to_all(parts, axis, split_axis=0, concat_axis=0, tiled=True)]
    all_to_all x2 -> x0, local copies, waits for them, and re-layouts: 12.9 us -> none  [the longest x1 12.4 us: per_device(): lax.all_to_all(features, FEAT, split_axis=0, concat_axis=1, tiled=True)]
    reduce_sum x13 -> x0, other arithmetic: 4.77 us -> none  [the longest x1 1.23 us: per_device(): jnp.sum(group_mom_new * group_mom_new - group_mom_old * group_mom_old)]
  transfers between devices with their start and end apart: 7 -> 0, of which waited for: 5 -> 0; matrix products, arithmetic and copies ran while one was open for 9% -> 0% of each run, Pallas kernels for 0% -> 0%
where the time goes in v1:
time: 155 us; the launch traced here: 154 us
  Pallas kernels  143 us (92%)
  local copies, waits for them, and re-layouts  6.75 us (4%)
  other arithmetic  4.27 us (3%)
    pallas_call x1, Pallas kernels, per_device(): pl.pallas_call(lambda *refs: kernel(rows_total, group_total, *refs), out_...  143 us

profile of v1, /device:TPU:1, one launch (start us, length us, event | category | flops | bytes accessed | tf_op | source)
XLA Modules:
  0.0 154.4 jit_solution(7847331936416073098)
XLA Ops:
  0.6 0.7 multiply_exponential_fusion
  1.3 0.1 fusion.4
  1.4 0.1 transpose.35
  1.4 0.1 transpose.36
  1.5 0.7 select_maximum_fusion.refs_5_
  2.2 0.8 copy.13
  3.0 1.5 maximum_maximum_fusion.refs_3_
  4.5 0.8 copy.14
  5.3 1.5 maximum_maximum_fusion.1.refs_4_
  6.8 142.7 %leapfrog.1 = (f32[96,128]{1,0:T(8,128)}, f32[96,128]{1,0:T(8,128)}, f32[8,128]{1,0:T(8,128)}) custom-call(bf16[32768,128]{1,0:T(8,128)(2,1)} %refs_0_.1, s32[256,128]{1,0:T(8,128)} %bitcast.15, s32[256,128]{1,0:T(8,128)} %bitcast.16, f32[96,128]{1,0:T(8,128)} %maximum_maximum_fusion.refs_3_, f32[96,128]{1,0:T(8,128)} %maximum_maximum_fusion.1.refs_4_, ...), custom_call_target="tpu_custom_call" | custom-call | tf_op jit(solution)/shard_map/leapfrog/pallas_call | solution.py:397
  149.5 1.2 slice.60
  150.7 0.9 fusion
  151.5 1.4 slice_bitcast_fusion
  152.9 0.7 copy.16
  153.7 0.7 copy.15
  (4 shorter events, 0.0 us)

commit v2 on v1

v2 whole, which is shorter than its diff:
```python
import math

import jax
import jax.numpy as jnp
from jax import lax
from jax.experimental import pallas as pl
from jax.experimental.pallas import tpu as pltpu
from jax.sharding import Mesh
from jax.sharding import PartitionSpec as P

FEAT = ("feat_0", "feat_1")
DP = ("dp_0", "dp_1")

NC = 4
LANES = 1024 // NC
CHUNK = 4 * LANES
BLOCK = NC * CHUNK
AHEAD = 1
BF16, F32 = jnp.bfloat16, jnp.float32


def dot(a, b):
    return lax.dot_general(a, b, (((1,), (0,)), ((), ())), preferred_element_type=F32)


def kernel(rows_total, group_total, feats, labels, groups, coef_ref, coef_mom_ref, group_ref, group_mom_ref,
           scale_ref, coef_out, coef_mom_out, group_out, group_mom_out, energy_ref,
           X, ST, XO, OHT, W, PL, R1, R2, RG, CS, CG, ACC, GS, GR, DA, DAR, DB, DC, EN, LL, DIFF,
           POS, MOM, IV, HALF, NEW, WIDE,
           loc_sem, a_s, a_r, rs_s, rs_r, g_s, g_r, c_s, c_r, q_s, q_r, d_s, d_r, e_s, e_r):
    x, core = lax.axis_index("dp_0"), lax.axis_index("dp_1")
    place = (lax.axis_index("feat_0"), lax.axis_index("feat_1"))
    classes = coef_ref.shape[0]

    def at(axis, step):
        return {FEAT[axis]: lax.rem(place[axis] + step, 4)}

    def feat_at(k):
        return {**at(0, k // 4), **at(1, k % 4)}

    def dp_at(k):
        return {"dp_0": lax.rem(x + k, 4)} if k else {"dp_1": 1 - core}

    def remote(src, dst, s, r, device):
        return pltpu.make_async_remote_copy(
            src_ref=src, dst_ref=dst, send_sem=s, recv_sem=r,
            device_id=device, device_id_type=pl.DeviceIdType.MESH)

    def a2a(t, c, k):
        me = place[t]
        half = CHUNK // 2

        def rows(step, part, count):
            first = (t * 4 + lax.rem(me + step, 4)) * BLOCK + c * CHUNK + part * half
            return feats.at[pl.ds(pl.multiple_of(first, half), count)]

        def to(r, part, count):
            return X.at[t, r, pl.ds(pl.multiple_of(c * CHUNK + part * half, half), count)]

        sems = (a_s.at[t, c, k], a_r.at[t, c, k])
        if k == 0:
            return remote(rows(1, 0, CHUNK), to(3, 0, CHUNK), *sems, at(t, 1))
        if k == 1:
            return remote(rows(3, 0, CHUNK), to(1, 0, CHUNK), *sems, at(t, 3))
        if k == 2:
            return remote(rows(2, 0, half), ST.at[t, c, 0], *sems, at(t, 1))
        if k == 3:
            return remote(rows(2, 1, half), ST.at[t, c, 1], *sems, at(t, 3))
        if k == 4:
            return remote(ST.at[t, c, 0], to(2, 0, half), *sems, at(t, 1))
        return remote(ST.at[t, c, 1], to(2, 1, half), *sems, at(t, 3))

    def scatter(e, t, c, k):
        axis = 1 - t
        p = place[axis]
        step = 1 if k % 2 == 0 else 3
        owner = lax.rem(p + (2 if k < 2 else step), 4)
        part = pl.ds((0, 1, 1, 0, 0, 1)[k] * 32, 32)
        dst = R1.at[e, t, c, k] if k < 2 else R2.at[e, t, c, k % 2, part]
        return remote(PL.at[e, t, c, owner, part], dst, rs_s.at[e, t, c, k], rs_r.at[e, t, c, k], at(axis, step))

    def gather(e, t, c, k):
        axis = 1 - t
        p = place[axis]
        step = 1 if k % 2 == 0 else 3
        ref = RG.at[e, t, c, p] if k < 2 else RG.at[e, t, c, lax.rem(p + 4 - step, 4), pl.ds((k - 2) * 32, 32)]
        return remote(ref, ref, g_s.at[e, t, c, k], g_r.at[e, t, c, k], at(axis, step))

    def weights(e, t, r):
        return remote(CS.at[e], CG.at[e, t, 3 - r], c_s.at[e, t, r - 1], c_r.at[e, t, r - 1], at(t, r))

    def gradients(e, t, r):
        return remote(GS.at[e, t, r], GR.at[e, t, r - 1], q_s.at[e, t, r - 1], q_r.at[e, t, r - 1], at(t, r))

    def dp_sum(e, k):
        sems = (d_s.at[e, k], d_r.at[e, k])
        if k == 0:
            return remote(DA.at[e, 1 - core], DAR.at[e], *sems, dp_at(0))
        if k < 4:
            return remote(DB.at[e, x], DB.at[e, x], *sems, dp_at(k))
        return remote(DC.at[e, core], DC.at[e, core], *sems, dp_at(0))

    def energies(k):
        mine = place[0] * 4 + place[1]
        return remote(EN.at[mine], EN.at[mine], e_s.at[k - 1], e_r.at[k - 1], feat_at(k))

    def own(t):
        first = (t * 4 + place[t]) * BLOCK
        return pltpu.make_async_copy(feats.at[pl.ds(pl.multiple_of(first, BLOCK), BLOCK)], X.at[t, 0], loc_sem.at[t])

    lane = lax.broadcasted_iota(jnp.int32, (32, 128), 1)
    low = lane < 64

    @jax.named_call
    def enter():
        barrier = pltpu.get_barrier_semaphore()
        for k in range(1, 16):
            pl.semaphore_signal(barrier, inc=1, device_id=feat_at(k), device_id_type=pl.DeviceIdType.MESH)
        for k in range(4):
            pl.semaphore_signal(barrier, inc=1, device_id=dp_at(k), device_id_type=pl.DeviceIdType.MESH)
        pl.semaphore_wait(barrier, 19)

    def pack(square):
        WIDE[:, 0:64] = square
        wide = WIDE[...]
        return jnp.concatenate([wide, pltpu.roll(wide, 96, 1)], axis=0).T[:32]

    def unpack(both):
        tall = jnp.concatenate([both, jnp.zeros((96, 128), F32)], axis=0).T
        return jnp.where(lax.broadcasted_iota(jnp.int32, (64, 128), 1) < 32, tall[:64], pltpu.roll(tall[64:], 32, 1))[:, :64]

    @jax.named_call
    def prepare():
        WIDE[...] = jnp.zeros_like(WIDE)
        POS[0:64], POS[64:96] = coef_ref[...], pack(group_ref[...])
        CS[0] = POS[...].astype(BF16)
        MOM[0:64], MOM[64:96] = coef_mom_ref[...], pack(group_mom_ref[...])
        IV[0:64] = jnp.ones((64, 128), F32)
        IV[64:96] = pack(jnp.broadcast_to(jnp.exp(-2.0 * scale_ref[...]), (64, 64)))

    @jax.named_call
    def send_weights(e):
        for t in range(2):
            for r in (2, 1, 3):
                weights(e, t, r).start()

    @jax.named_call
    def gather_weights(e):
        for t in range(2):
            for r in (1, 3, 2):
                weights(e, t, r).wait_recv()
            packed = []
            for r in range(4):
                block = CS[e] if r == 0 else CG[e, t, r - 1]
                W[t, :, r * 128:(r + 1) * 128] = block[:classes]
                packed.append(block[classes:].astype(F32))
            for i in range(2):
                a, b = packed[2 * i], packed[2 * i + 1]
                lanes = pl.ds(512 + i * 128, 128)
                W[t, 0:32, lanes] = jnp.where(low, a, pltpu.roll(b, 64, 1)).astype(BF16)
                W[t, 32:64, lanes] = jnp.where(low, pltpu.roll(a, 64, 1), b).astype(BF16)

    @jax.named_call
    def onehots():
        ids = lax.broadcasted_iota(jnp.int32, (64, 128), 0)
        for t in range(2):
            def onehot(c, _):
                for h in range(CHUNK // 128):
                    group = groups[pl.ds(((t * 4 + place[t]) * NC + c) * (CHUNK // 128) + h, 1), :]
                    for r in range(4):
                        other = lax.rem(place[t] + r, 4)
                        owner = other * 4 + place[1] if t == 0 else place[0] * 4 + other
                        hit = ids + owner * 64 == group
                        XO[t, c, 512 + r * 64:512 + (r + 1) * 64, h * 128:(h + 1) * 128] = \
                            jnp.where(hit, 1.0, 0.0).astype(BF16)
                OHT[t, c] = XO[t, c, 512:768].T
                return 0
            lax.fori_loop(0, NC, onehot, 0)

    @jax.named_call
    def send_features(c):
        for k in (2, 3, 0, 1):
            for t in range(2):
                a2a(t, c, k).start()

    @jax.named_call
    def pass_features(c):
        for k in (2, 3):
            for t in range(2):
                a2a(t, c, k).wait_recv()
                a2a(t, c, k + 2).start()

    @jax.named_call
    def wait_features(c):
        for k in (0, 1, 4, 5):
            for t in range(2):
                a2a(t, c, k).wait_recv()

    def rows_of(c):
        return pl.ds(pl.multiple_of(c * CHUNK, CHUNK), CHUNK)

    @jax.named_call
    def turn(c):
        for t in range(2):
            for r in range(4):
                XO[t, c, r * 128:(r + 1) * 128] = X[t, r, rows_of(c), :].T

    @jax.named_call
    def logits(e, c):
        for t in range(2):
            total = dot(W[t], XO[t, c])
            for o in range(4):
                PL[e, t, c, o] = total[:, o * LANES:(o + 1) * LANES]
            for k in range(4):
                scatter(e, t, c, k).start()

    @jax.named_call
    def add_passed(e, c):
        for t in range(2):
            p = place[1 - t]
            for k in range(2):
                scatter(e, t, c, k).wait_recv()
                owner = lax.rem(p + (1 if k == 0 else 3), 4)
                part = pl.ds(k * 32, 32)
                PL[e, t, c, owner, part] = PL[e, t, c, owner, part] + R1[e, t, c, k]
            for k in (4, 5):
                scatter(e, t, c, k).start()

    @jax.named_call
    def softmax(e, c):
        for t in range(2):
            p = place[1 - t]
            for k in range(2, 6):
                scatter(e, t, c, k).wait_recv()
            value = PL[e, t, c, p] + R2[e, t, c, 0] + R2[e, t, c, 1]
            first = (((t * 4 + place[t]) * NC + c) * 4 + p) * (LANES // 128)
            label = jnp.concatenate([labels[pl.ds(first + i, 1), :] for i in range(LANES // 128)], axis=1)
            shifted = value - jnp.max(value, axis=0, keepdims=True)
            scaled = jnp.exp(shifted)
            normalizer = jnp.sum(scaled, axis=0, keepdims=True)
            hit = lax.broadcasted_iota(jnp.int32, value.shape, 0) == label
            probability = scaled * (1.0 / normalizer)
            RG[e, t, c, p] = (jnp.where(hit, 1.0, 0.0) - probability).astype(BF16)
            for k in range(2):
                gather(e, t, c, k).start()
            loglik = jnp.sum(jnp.where(hit, shifted, 0.0), axis=0, keepdims=True) - jnp.log(normalizer)
            if e == 0:
                LL[t, c] = jnp.broadcast_to(loglik, (8, LANES))
            else:
                change = LL[t, c] - loglik
                for i in range(LANES // 128):
                    DIFF[...] = DIFF[...] + change[:, i * 128:(i + 1) * 128]

    @jax.named_call
    def pass_residual(e, c):
        for t in range(2):
            for k in range(2):
                gather(e, t, c, k).wait_recv()
                gather(e, t, c, k + 2).start()

    @jax.named_call
    def gradient(e, c):
        for t in range(2):
            for k in (2, 3):
                gather(e, t, c, k).wait_recv()

            rows = rows_of(c)
            res = jnp.concatenate([RG[e, t, c, o] for o in range(4)], axis=1)
            for r in (0, 2):
                two = jnp.concatenate([X[t, r, rows, :], X[t, r + 1, rows, :]], axis=1)
                ACC[t, :, r * 128:(r + 2) * 128] += dot(res, two)
            ACC[t, :, 512:768] += dot(res, OHT[t, c])

    @jax.named_call
    def ring_sum(e):
        for r in (2, 1, 3, 0):
            for t in range(2):
                GS[e, t, r, 0:classes] = ACC[t, :, r * 128:(r + 1) * 128]
                tile = 512 + (r // 2) * 128
                top, bottom = ACC[t, 0:32, tile:tile + 128], ACC[t, 32:64, tile:tile + 128]
                if r % 2 == 0:
                    GS[e, t, r, classes:] = jnp.where(low, top, pltpu.roll(bottom, 64, 1))
                else:
                    GS[e, t, r, classes:] = jnp.where(low, pltpu.roll(top, 64, 1), bottom)
                if r:
                    gradients(e, t, r).start()
        total = GS[e, 0, 0] + GS[e, 1, 0]
        for r in (1, 3, 2):
            for t in range(2):
                gradients(e, t, r).wait_recv()
                total = total + GR[e, t, r - 1]
        for h in range(2):
            DA[e, h, 0:48] = total[h * 48:(h + 1) * 48]
            DA[e, h, 48:56] = DIFF[...]

    @jax.named_call
    def core_sum(e):
        dp_sum(e, 0).start()
        dp_sum(e, 0).wait_recv()
        DB[e, x] = DA[e, core] + DAR[e]

    @jax.named_call
    def chip_sum(e):
        for k in (2, 1, 3):
            dp_sum(e, k).start()
        for k in (1, 3, 2):
            dp_sum(e, k).wait_recv()
        total = ((DB[e, 0] + DB[e, 1]) + DB[e, 2]) + DB[e, 3]
        DC[e, core] = total[0:48]
        return total[48:56]

    @jax.named_call
    def core_share(e):
        dp_sum(e, 4).start()
        dp_sum(e, 4).wait_recv()
        return jnp.concatenate([DC[e, 0], DC[e, 1]], axis=0)

    def total_gradient(e):
        ring_sum(e)
        core_sum(e)
        change = chip_sum(e)
        return core_share(e), change

    row = lax.broadcasted_iota(jnp.int32, (96, 128), 0)
    step = jnp.where(row < classes, 4.0 / math.sqrt(rows_total), 4.0 * math.sqrt(group_total / rows_total))

    @jax.named_call
    def left(e):
        def over(c, _):
            for t in range(2):
                for k in range(6):
                    if e == 0:
                        a2a(t, c, k).wait_send()
                    scatter(e, t, c, k).wait_send()
                    if k < 4:
                        gather(e, t, c, k).wait_send()
            return 0
        lax.fori_loop(0, NC, over, 0)
        for t in range(2):
            for r in range(1, 4):
                weights(e, t, r).wait_send()
                gradients(e, t, r).wait_send()
        for k in range(5):
            dp_sum(e, k).wait_send()

    def stages(s, table):
        for lag, body in table:
            c = s - lag
            pl.when(jnp.logical_and(c >= 0, c < NC))(lambda c=c, body=body: body(c))

    own(0).start()
    own(1).start()
    enter()
    for c in range(AHEAD):
        send_features(c)
    prepare()
    send_weights(0)
    DIFF[...] = jnp.zeros_like(DIFF)
    ACC[...] = jnp.zeros_like(ACC)
    onehots()
    gather_weights(0)
    own(0).wait()
    own(1).wait()

    def arrived(c):
        wait_features(c)
        turn(c)
        logits(0, c)

    def first_slot(s, _):
        stages(s, (
            (-AHEAD, send_features),
            (0, pass_features),
            (1, arrived),
            (2, lambda c: add_passed(0, c)),
            (3, lambda c: softmax(0, c)),
            (4, lambda c: pass_residual(0, c)),
            (5, lambda c: gradient(0, c)),
        ))
        return 0
    lax.fori_loop(0, NC + 5, first_slot, 0)

    grad, _ = total_gradient(0)
    half = MOM[...] + 0.5 * step * (grad - POS[...] * IV[...])
    new = POS[...] + step * half
    CS[1] = new.astype(BF16)
    send_weights(1)
    HALF[...] = half
    NEW[...] = new
    coef_out[...] = new[:classes]
    group_out[...] = unpack(new[classes:])
    left(0)

    ACC[...] = jnp.zeros_like(ACC)
    gather_weights(1)

    def over(body):
        def step_of(c, _):
            body(1, c)
            return 0
        lax.fori_loop(0, NC, step_of, 0)

    over(logits)
    over(add_passed)
    over(softmax)

    def last_slot(s, _):
        stages(s, ((0, lambda c: pass_residual(1, c)), (3, lambda c: gradient(1, c))))
        return 0
    lax.fori_loop(0, NC + 3, last_slot, 0)

    grad, change = total_gradient(1)

    @jax.named_call
    def finish():
        half, new = HALF[...], NEW[...]
        mom = half + 0.5 * step * (grad - new * IV[...])
        state = 0.5 * ((new * new - POS[...] * POS[...]) * IV[...] + (mom * mom - MOM[...] * MOM[...]))
        EN[place[0] * 4 + place[1]] = change + jnp.sum(state, axis=0, keepdims=True)
        for k in range(1, 16):
            energies(k).start()
        coef_mom_out[...] = mom[:classes]
        group_mom_out[...] = unpack(mom[classes:])
    finish()
    left(1)

    @jax.named_call
    def total_energy():
        for k in range(1, 16):
            energies(k).wait_recv()
        terms = EN[0]
        for i in range(1, 16):
            terms = terms + EN[i]
        energy_ref[...] = jnp.broadcast_to(jnp.sum(terms, axis=1, keepdims=True), (8, 128))
        for k in range(1, 16):
            energies(k).wait_send()
    total_energy()


def hand_over(*refs):
    for source, target in zip(refs[:5], refs[5:]):
        target[...] = source[0:1, 0:1] if target.shape == (1, 1) else source[...]


def per_device(
    features, labels, groups, coefficients, coef_momentum, group_effects, group_momentum, log_scale
):
    rows = labels.shape[0]
    classes = coefficients.shape[1]
    rows_total = rows * lax.axis_size(DP)
    group_total = group_effects.shape[0] * lax.axis_size(FEAT)
    vmem = pl.BlockSpec(memory_space=pltpu.VMEM)
    dma = pltpu.SemaphoreType.DMA
    shapes = [(64, 128), (64, 128), (64, 64), (64, 64)]
    results = pl.pallas_call(
        lambda *refs: kernel(rows_total, group_total, *refs),
        out_shape=[jax.ShapeDtypeStruct(s, F32) for s in shapes + [(8, 128)]],
        in_specs=[pl.BlockSpec(memory_space=pl.ANY)] + [vmem] * 7,
        out_specs=[vmem] * 5,
        scratch_shapes=[
            pltpu.VMEM((2, 4, BLOCK, 128), BF16),
            pltpu.VMEM((2, NC, 2, CHUNK // 2, 128), BF16),
            pltpu.VMEM((2, NC, 768, CHUNK), BF16),
            pltpu.VMEM((2, NC, CHUNK, 256), BF16),
            pltpu.VMEM((2, 64, 768), BF16),
            pltpu.VMEM((2, 2, NC, 4, 64, LANES), F32),
            pltpu.VMEM((2, 2, NC, 2, 32, LANES), F32),
            pltpu.VMEM((2, 2, NC, 2, 64, LANES), F32),
            pltpu.VMEM((2, 2, NC, 4, 64, LANES), BF16),
            pltpu.VMEM((2, 96, 128), BF16),
            pltpu.VMEM((2, 2, 3, 96, 128), BF16),
            pltpu.VMEM((2, 64, 768), F32),
            pltpu.VMEM((2, 2, 4, 96, 128), F32),
            pltpu.VMEM((2, 2, 3, 96, 128), F32),
            pltpu.VMEM((2, 2, 56, 128), F32),
            pltpu.VMEM((2, 56, 128), F32),
            pltpu.VMEM((2, 4, 56, 128), F32),
            pltpu.VMEM((2, 2, 48, 128), F32),
            pltpu.VMEM((16, 8, 128), F32),
            pltpu.VMEM((2, NC, 8, LANES), F32),
            pltpu.VMEM((8, 128), F32),
            pltpu.VMEM((96, 128), F32), pltpu.VMEM((96, 128), F32), pltpu.VMEM((96, 128), F32),
            pltpu.VMEM((96, 128), F32), pltpu.VMEM((96, 128), F32),
            pltpu.VMEM((64, 128), F32),
            dma((2,)),
            dma((2, NC, 6)), dma((2, NC, 6)),
            dma((2, 2, NC, 6)), dma((2, 2, NC, 6)),
            dma((2, 2, NC, 4)), dma((2, 2, NC, 4)),
            dma((2, 2, 3)), dma((2, 2, 3)),
            dma((2, 2, 3)), dma((2, 2, 3)),
            dma((2, 5)), dma((2, 5)),
            dma((15,)), dma((15,)),
        ],
        compiler_params=pltpu.CompilerParams(
            collective_id=0, has_side_effects=True, vmem_limit_bytes=58 * 2**20),
        name="leapfrog",
    )(features, labels.reshape(-1, 128), groups.reshape(-1, 128), coefficients.T, coef_momentum.T,
      group_effects, group_momentum, log_scale.reshape(1, -1))
    coef, coef_mom, group, group_mom, energy = pl.pallas_call(
        hand_over,
        out_shape=[jax.ShapeDtypeStruct(s, F32) for s in shapes + [(1, 1)]],
        in_specs=[vmem] * 5,
        out_specs=[vmem] * 5,
        name="hand_over",
    )(*results)
    return (coef.T, coef_mom.T, group, group_mom, energy[0, 0])


def solution(mesh):
    torus = Mesh(mesh.devices.reshape(4, 2, 4, 4), ("dp_0", "dp_1", "feat_0", "feat_1"))
    in_specs = (
        P(DP, FEAT),
        P(DP),
        P(DP),
        P(FEAT, None),
        P(FEAT, None),
        P(FEAT, None),
        P(FEAT, None),
        P(),
    )
    out_specs = (P(FEAT, None), P(FEAT, None), P(FEAT, None), P(FEAT, None), P())
    return jax.shard_map(
        per_device, mesh=torus, in_specs=in_specs, out_specs=out_specs, check_vma=False
    )
```

time: 155 us -> 135 us (0.87)
  Pallas kernels: 143 us -> 134 us
  local copies, waits for them, and re-layouts: 6.75 us -> 0 us
  other arithmetic: 4.27 us -> 0 us
    pallas_call x1, Pallas kernels: 143 us -> 132 us  [per_device(): pl.pallas_call(lambda *refs: kernel(rows_total, group_total, *refs), out_...]
    concatenate x3 -> x0, other arithmetic: 3.6 us -> none  [the longest x2 2.9 us: packed(): jnp.concatenate([coef.T, jnp.concatenate([turned[:32], turned[32:]], axis...]
    unnamed x4 -> x0, local copies, waits for them, and re-layouts: 3.06 us -> none
    slice x5 -> x0, local copies, waits for them, and re-layouts: 2.14 us -> none  [the longest x1 1.19 us: per_device(): return (new_coef, new_coef_mom, new_group, new_group_mom, energy[0, 0])]
where the time goes in v2:
time: 135 us
  Pallas kernels  134 us (99%)
    pallas_call x1, Pallas kernels, per_device(): pl.pallas_call(lambda *refs: kernel(rows_total, group_total, *refs), out_...  132 us

profile of v2, /device:TPU:1, one launch (start us, length us, event | category | flops | bytes accessed | tf_op | source)
XLA Modules:
  0.0 134.5 jit_solution(13719568289445383086)
XLA Ops:
  0.6 132.4 %leapfrog.1 = (f32[64,128]{1,0:T(8,128)}, f32[64,128]{1,0:T(8,128)}, f32[64,64]{1,0:T(8,128)}, f32[64,64]{1,0:T(8,128)}, f32[8,128]{1,0:T(8,128)}) custom-call(bf16[32768,128]{1,0:T(8,128)(2,1)} %refs_0_.1, s32[256,128]{1,0:T(8,128)} %bitcast.8, s32[256,128]{1,0:T(8,128)} %bitcast.9, f32[64,128]{1,0:T(8,128)} %bitcast.10, f32[64,128]{1,0:T(8,128)} %bitcast.11, ...), custom_call_target="tpu_custom_call" | custom-call | tf_op jit(solution)/shard_map/leapfrog/pallas_call | solution.py:455
  133.1 1.5 %hand_over.1 = (f32[64,128]{1,0:T(8,128)}, f32[64,128]{1,0:T(8,128)}, f32[64,64]{1,0:T(8,128)}, f32[64,64]{1,0:T(8,128)}, f32[1,1]{1,0:T(1,128)}) custom-call(f32[64,128]{1,0:T(8,128)} %get-tuple-element.15.refs_0_, f32[64,128]{1,0:T(8,128)} %get-tuple-element.16.refs_1_, f32[64,64]{1,0:T(8,128)} %get-tuple-element.17.refs_2_, ...), custom_call_target="tpu_custom_call" | custom-call | tf_op jit(solution)/shard_map/hand_over/pallas_call | solution.py:499

commit v3 on v2

--- a/solution.py
+++ b/solution.py
@@ -23,11 +23,17 @@
     return lax.dot_general(a, b, (((1,), (0,)), ((), ())), preferred_element_type=F32)
 
 
-def kernel(rows_total, group_total, feats, labels, groups, coef_ref, coef_mom_ref, group_ref, group_mom_ref,
-           scale_ref, coef_out, coef_mom_out, group_out, group_mom_out, energy_ref,
+def kernel(rows_total, group_total, *refs):
+    feats, sources, targets, rest = refs[0], refs[1:8], refs[8:13], refs[13:]
+    body(rows_total, group_total, feats, sources, targets, *rest)
+
+
+def body(rows_total, group_total, feats, sources, targets,
+           labels, groups, coef_ref, coef_mom_ref, group_ref, group_mom_ref, scale_ref,
+           coef_out, coef_mom_out, group_out, group_mom_out, energy_ref,
            X, ST, XO, OHT, W, PL, R1, R2, RG, CS, CG, ACC, GS, GR, DA, DAR, DB, DC, EN, LL, DIFF,
            POS, MOM, IV, HALF, NEW, WIDE,
-           loc_sem, a_s, a_r, rs_s, rs_r, g_s, g_r, c_s, c_r, q_s, q_r, d_s, d_r, e_s, e_r):
+           loc_sem, in_sem, out_sem, a_s, a_r, rs_s, rs_r, g_s, g_r, c_s, c_r, q_s, q_r, d_s, d_r, e_s, e_r):
     x, core = lax.axis_index("dp_0"), lax.axis_index("dp_1")
     place = (lax.axis_index("feat_0"), lax.axis_index("feat_1"))
     classes = coef_ref.shape[0]
@@ -57,7 +63,7 @@
         def to(r, part, count):
             return X.at[t, r, pl.ds(pl.multiple_of(c * CHUNK + part * half, half), count)]
 
-        sems = (a_s.at[t, c, k], a_r.at[t, c, k])
+        sems = (a_s.at[0], a_r.at[t, c, 1 if k in (2, 3) else 0])
         if k == 0:
             return remote(rows(1, 0, CHUNK), to(3, 0, CHUNK), *sems, at(t, 1))
         if k == 1:
@@ -77,23 +83,23 @@
         owner = lax.rem(p + (2 if k < 2 else step), 4)
         part = pl.ds((0, 1, 1, 0, 0, 1)[k] * 32, 32)
         dst = R1.at[e, t, c, k] if k < 2 else R2.at[e, t, c, k % 2, part]
-        return remote(PL.at[e, t, c, owner, part], dst, rs_s.at[e, t, c, k], rs_r.at[e, t, c, k], at(axis, step))
+        return remote(PL.at[e, t, c, owner, part], dst, rs_s.at[e], rs_r.at[e, t, c, 0 if k < 2 else 1], at(axis, step))
 
     def gather(e, t, c, k):
         axis = 1 - t
         p = place[axis]
         step = 1 if k % 2 == 0 else 3
         ref = RG.at[e, t, c, p] if k < 2 else RG.at[e, t, c, lax.rem(p + 4 - step, 4), pl.ds((k - 2) * 32, 32)]
-        return remote(ref, ref, g_s.at[e, t, c, k], g_r.at[e, t, c, k], at(axis, step))
+        return remote(ref, ref, g_s.at[e], g_r.at[e, t, c, k // 2], at(axis, step))
 
     def weights(e, t, r):
-        return remote(CS.at[e], CG.at[e, t, 3 - r], c_s.at[e, t, r - 1], c_r.at[e, t, r - 1], at(t, r))
+        return remote(CS.at[e], CG.at[e, t, 3 - r], c_s.at[e], c_r.at[e, t], at(t, r))
 
     def gradients(e, t, r):
-        return remote(GS.at[e, t, r], GR.at[e, t, r - 1], q_s.at[e, t, r - 1], q_r.at[e, t, r - 1], at(t, r))
+        return remote(GS.at[e, t, r], GR.at[e, t, r - 1], q_s.at[e], q_r.at[e, t], at(t, r))
 
     def dp_sum(e, k):
-        sems = (d_s.at[e, k], d_r.at[e, k])
+        sems = (d_s.at[e], d_r.at[e, (0, 1, 1, 1, 2)[k]])
         if k == 0:
             return remote(DA.at[e, 1 - core], DAR.at[e], *sems, dp_at(0))
         if k < 4:
@@ -102,23 +108,39 @@
 
     def energies(k):
         mine = place[0] * 4 + place[1]
-        return remote(EN.at[mine], EN.at[mine], e_s.at[k - 1], e_r.at[k - 1], feat_at(k))
+        return remote(EN.at[mine], EN.at[mine], e_s.at[0], e_r.at[0], feat_at(k))
+
+    def bytes_of(ref, sem):
+        pltpu.make_async_copy(ref, ref, sem).wait()
 
     def own(t):
         first = (t * 4 + place[t]) * BLOCK
         return pltpu.make_async_copy(feats.at[pl.ds(pl.multiple_of(first, BLOCK), BLOCK)], X.at[t, 0], loc_sem.at[t])
 
+    def fetch(i):
+        local = (labels, groups, coef_ref, coef_mom_ref, group_ref, group_mom_ref, scale_ref)[i]
+        return pltpu.make_async_copy(sources[i], local, in_sem.at[i])
+
+    def store(i):
+        local = (coef_out, coef_mom_out, group_out, group_mom_out, energy_ref)[i]
+        return pltpu.make_async_copy(local, targets[i], out_sem.at[i])
+
     lane = lax.broadcasted_iota(jnp.int32, (32, 128), 1)
     low = lane < 64
 
+    barrier = pltpu.get_barrier_semaphore()
+
     @jax.named_call
     def enter():
-        barrier = pltpu.get_barrier_semaphore()
-        for k in range(1, 16):
-            pl.semaphore_signal(barrier, inc=1, device_id=feat_at(k), device_id_type=pl.DeviceIdType.MESH)
-        for k in range(4):
-            pl.semaphore_signal(barrier, inc=1, device_id=dp_at(k), device_id_type=pl.DeviceIdType.MESH)
-        pl.semaphore_wait(barrier, 19)
+        peers = [at(axis, k) for axis in range(2) for k in range(1, 4)] + [dp_at(k) for k in range(4)]
+        for peer in peers:
+            pl.semaphore_signal(barrier, inc=1, device_id=peer, device_id_type=pl.DeviceIdType.MESH)
+        for i in (2, 4, 3, 5, 6, 0, 1):
+            fetch(i).start()
+
+    @jax.named_call
+    def met():
+        pl.semaphore_wait(barrier, 10)
 
     def pack(square):
         WIDE[:, 0:64] = square
@@ -132,6 +154,10 @@
     @jax.named_call
     def prepare():
         WIDE[...] = jnp.zeros_like(WIDE)
+        DIFF[...] = jnp.zeros_like(DIFF)
+        ACC[...] = jnp.zeros_like(ACC)
+        for i in (2, 4, 3, 5, 6):
+            fetch(i).wait()
         POS[0:64], POS[64:96] = coef_ref[...], pack(group_ref[...])
         CS[0] = POS[...].astype(BF16)
         MOM[0:64], MOM[64:96] = coef_mom_ref[...], pack(group_mom_ref[...])
@@ -147,8 +173,7 @@
     @jax.named_call
     def gather_weights(e):
         for t in range(2):
-            for r in (1, 3, 2):
-                weights(e, t, r).wait_recv()
+            bytes_of(CG.at[e, t], c_r.at[e, t])
             packed = []
             for r in range(4):
                 block = CS[e] if r == 0 else CG[e, t, r - 1]
@@ -185,16 +210,15 @@
 
     @jax.named_call
     def pass_features(c):
-        for k in (2, 3):
-            for t in range(2):
-                a2a(t, c, k).wait_recv()
-                a2a(t, c, k + 2).start()
+        for t in range(2):
+            bytes_of(ST.at[t, c], a_r.at[t, c, 1])
+            a2a(t, c, 4).start()
+            a2a(t, c, 5).start()
 
     @jax.named_call
     def wait_features(c):
-        for k in (0, 1, 4, 5):
-            for t in range(2):
-                a2a(t, c, k).wait_recv()
+        for t in range(2):
+            bytes_of(X.at[t, pl.ds(1, 3), rows_of(c)], a_r.at[t, c, 0])
 
     def rows_of(c):
         return pl.ds(pl.multiple_of(c * CHUNK, CHUNK), CHUNK)
@@ -218,8 +242,8 @@
     def add_passed(e, c):
         for t in range(2):
             p = place[1 - t]
+            bytes_of(R1.at[e, t, c], rs_r.at[e, t, c, 0])
             for k in range(2):
-                scatter(e, t, c, k).wait_recv()
                 owner = lax.rem(p + (1 if k == 0 else 3), 4)
                 part = pl.ds(k * 32, 32)
                 PL[e, t, c, owner, part] = PL[e, t, c, owner, part] + R1[e, t, c, k]
@@ -230,8 +254,7 @@
     def softmax(e, c):
         for t in range(2):
             p = place[1 - t]
-            for k in range(2, 6):
-                scatter(e, t, c, k).wait_recv()
+            bytes_of(R2.at[e, t, c], rs_r.at[e, t, c, 1])
             value = PL[e, t, c, p] + R2[e, t, c, 0] + R2[e, t, c, 1]
             first = (((t * 4 + place[t]) * NC + c) * 4 + p) * (LANES // 128)
             label = jnp.concatenate([labels[pl.ds(first + i, 1), :] for i in range(LANES // 128)], axis=1)
@@ -254,15 +277,14 @@
     @jax.named_call
     def pass_residual(e, c):
         for t in range(2):
-            for k in range(2):
-                gather(e, t, c, k).wait_recv()
-                gather(e, t, c, k + 2).start()
+            bytes_of(RG.at[e, t, c, pl.ds(0, 2)], g_r.at[e, t, c, 0])
+            gather(e, t, c, 2).start()
+            gather(e, t, c, 3).start()
 
     @jax.named_call
     def gradient(e, c):
         for t in range(2):
-            for k in (2, 3):
-                gather(e, t, c, k).wait_recv()
+            bytes_of(RG.at[e, t, c, 0], g_r.at[e, t, c, 1])
 
             rows = rows_of(c)
             res = jnp.concatenate([RG[e, t, c, o] for o in range(4)], axis=1)
@@ -285,10 +307,10 @@
                 if r:
                     gradients(e, t, r).start()
         total = GS[e, 0, 0] + GS[e, 1, 0]
-        for r in (1, 3, 2):
-            for t in range(2):
-                gradients(e, t, r).wait_recv()
-                total = total + GR[e, t, r - 1]
+        for t in range(2):
+            bytes_of(GR.at[e, t], q_r.at[e, t])
+            for r in range(3):
+                total = total + GR[e, t, r]
         for h in range(2):
             DA[e, h, 0:48] = total[h * 48:(h + 1) * 48]
             DA[e, h, 48:56] = DIFF[...]
@@ -303,8 +325,7 @@
     def chip_sum(e):
         for k in (2, 1, 3):
             dp_sum(e, k).start()
-        for k in (1, 3, 2):
-            dp_sum(e, k).wait_recv()
+        bytes_of(DB.at[e, pl.ds(0, 3)], d_r.at[e, 1])
         total = ((DB[e, 0] + DB[e, 1]) + DB[e, 2]) + DB[e, 3]
         DC[e, core] = total[0:48]
         return total[48:56]
@@ -326,37 +347,30 @@
 
     @jax.named_call
     def left(e):
-        def over(c, _):
-            for t in range(2):
-                for k in range(6):
-                    if e == 0:
-                        a2a(t, c, k).wait_send()
-                    scatter(e, t, c, k).wait_send()
-                    if k < 4:
-                        gather(e, t, c, k).wait_send()
-            return 0
-        lax.fori_loop(0, NC, over, 0)
-        for t in range(2):
-            for r in range(1, 4):
-                weights(e, t, r).wait_send()
-                gradients(e, t, r).wait_send()
-        for k in range(5):
-            dp_sum(e, k).wait_send()
+        if e == 0:
+            bytes_of(X, a_s.at[0])
+        most = pl.ds(0, NC * 3 // 4)
+        bytes_of(PL.at[e, :, most], rs_s.at[e])
+        bytes_of(RG.at[e, :, most], g_s.at[e])
+        bytes_of(CG.at[e], c_s.at[e])
+        bytes_of(GR.at[e], q_s.at[e])
+        bytes_of(X.at[0, 0, pl.ds(0, 2 * (4 * 56 + 48))], d_s.at[e])
 
     def stages(s, table):
         for lag, body in table:
             c = s - lag
             pl.when(jnp.logical_and(c >= 0, c < NC))(lambda c=c, body=body: body(c))
 
+    enter()
+    prepare()
+    met()
+    send_weights(0)
+    for c in range(AHEAD):
+        send_features(c)
     own(0).start()
     own(1).start()
-    enter()
-    for c in range(AHEAD):
-        send_features(c)
-    prepare()
-    send_weights(0)
-    DIFF[...] = jnp.zeros_like(DIFF)
-    ACC[...] = jnp.zeros_like(ACC)
+    fetch(0).wait()
+    fetch(1).wait()
     onehots()
     gather_weights(0)
     own(0).wait()
@@ -389,6 +403,8 @@
     NEW[...] = new
     coef_out[...] = new[:classes]
     group_out[...] = unpack(new[classes:])
+    store(0).start()
+    store(2).start()
     left(0)
 
     ACC[...] = jnp.zeros_like(ACC)
@@ -421,19 +437,23 @@
             energies(k).start()
         coef_mom_out[...] = mom[:classes]
         group_mom_out[...] = unpack(mom[classes:])
+        store(1).start()
+        store(3).start()
     finish()
     left(1)
+    for i in range(4):
+        store(i).wait()
 
     @jax.named_call
     def total_energy():
-        for k in range(1, 16):
-            energies(k).wait_recv()
+        bytes_of(EN.at[pl.ds(0, 15)], e_r.at[0])
         terms = EN[0]
         for i in range(1, 16):
             terms = terms + EN[i]
         energy_ref[...] = jnp.broadcast_to(jnp.sum(terms, axis=1, keepdims=True), (8, 128))
-        for k in range(1, 16):
-            energies(k).wait_send()
+        store(4).start()
+        bytes_of(EN.at[pl.ds(0, 15)], e_s.at[0])
+        store(4).wait()
     total_energy()
 
 
@@ -455,9 +475,14 @@
     results = pl.pallas_call(
         lambda *refs: kernel(rows_total, group_total, *refs),
         out_shape=[jax.ShapeDtypeStruct(s, F32) for s in shapes + [(8, 128)]],
-        in_specs=[pl.BlockSpec(memory_space=pl.ANY)] + [vmem] * 7,
-        out_specs=[vmem] * 5,
+        in_specs=[pl.BlockSpec(memory_space=pl.ANY)] * 8,
+        out_specs=[pl.BlockSpec(memory_space=pl.ANY)] * 5,
         scratch_shapes=[
+            pltpu.VMEM((rows // 128, 128), jnp.int32), pltpu.VMEM((rows // 128, 128), jnp.int32),
+            pltpu.VMEM((64, 128), F32), pltpu.VMEM((64, 128), F32),
+            pltpu.VMEM((64, 64), F32), pltpu.VMEM((64, 64), F32), pltpu.VMEM((1, 64), F32),
+            pltpu.VMEM((64, 128), F32), pltpu.VMEM((64, 128), F32),
+            pltpu.VMEM((64, 64), F32), pltpu.VMEM((64, 64), F32), pltpu.VMEM((8, 128), F32),
             pltpu.VMEM((2, 4, BLOCK, 128), BF16),
             pltpu.VMEM((2, NC, 2, CHUNK // 2, 128), BF16),
             pltpu.VMEM((2, NC, 768, CHUNK), BF16),
@@ -482,14 +507,14 @@
             pltpu.VMEM((96, 128), F32), pltpu.VMEM((96, 128), F32), pltpu.VMEM((96, 128), F32),
             pltpu.VMEM((96, 128), F32), pltpu.VMEM((96, 128), F32),
             pltpu.VMEM((64, 128), F32),
-            dma((2,)),
-            dma((2, NC, 6)), dma((2, NC, 6)),
-            dma((2, 2, NC, 6)), dma((2, 2, NC, 6)),
-            dma((2, 2, NC, 4)), dma((2, 2, NC, 4)),
-            dma((2, 2, 3)), dma((2, 2, 3)),
-            dma((2, 2, 3)), dma((2, 2, 3)),
-            dma((2, 5)), dma((2, 5)),
-            dma((15,)), dma((15,)),
+            dma((2,)), dma((7,)), dma((5,)),
+            dma((1,)), dma((2, NC, 2)),
+            dma((2,)), dma((2, 2, NC, 2)),
+            dma((2,)), dma((2, 2, NC, 2)),
+            dma((2,)), dma((2, 2)),
+            dma((2,)), dma((2, 2)),
+            dma((2,)), dma((2, 3)),
+            dma((1,)), dma((1,)),
         ],
         compiler_params=pltpu.CompilerParams(
             collective_id=0, has_side_effects=True, vmem_limit_bytes=58 * 2**20),

time: 135 us -> 127 us (0.941)
  Pallas kernels: 134 us -> 126 us
    pallas_call x1, Pallas kernels: 132 us -> 125 us  [per_device(): pl.pallas_call(lambda *refs: kernel(rows_total, group_total, *refs), out_...]
where the time goes in v3:
time: 127 us
  Pallas kernels  126 us (99%)
    pallas_call x1, Pallas kernels, per_device(): pl.pallas_call(lambda *refs: kernel(rows_total, group_total, *refs), out_...  125 us

profile of v3, /device:TPU:1, one launch (start us, length us, event | category | flops | bytes accessed | tf_op | source)
XLA Modules:
  0.0 127.0 jit_solution(4881880309690563440)
XLA Ops:
  0.6 124.9 %leapfrog.1 = (f32[64,128]{1,0:T(8,128)}, f32[64,128]{1,0:T(8,128)}, f32[64,64]{1,0:T(8,128)}, f32[64,64]{1,0:T(8,128)}, f32[8,128]{1,0:T(8,128)}) custom-call(bf16[32768,128]{1,0:T(8,128)(2,1)} %refs_0_.1, s32[256,128]{1,0:T(8,128)} %bitcast.8, s32[256,128]{1,0:T(8,128)} %bitcast.9, f32[64,128]{1,0:T(8,128)} %bitcast.10, f32[64,128]{1,0:T(8,128)} %bitcast.11, ...), custom_call_target="tpu_custom_call" | custom-call | tf_op jit(solution)/shard_map/leapfrog/pallas_call | solution.py:475
  125.5 1.5 %hand_over.1 = (f32[64,128]{1,0:T(8,128)}, f32[64,128]{1,0:T(8,128)}, f32[64,64]{1,0:T(8,128)}, f32[64,64]{1,0:T(8,128)}, f32[1,1]{1,0:T(1,128)}) custom-call(f32[64,128]{1,0:T(8,128)} %get-tuple-element.15.refs_0_, f32[64,128]{1,0:T(8,128)} %get-tuple-element.16.refs_1_, f32[64,64]{1,0:T(8,128)} %get-tuple-element.17.refs_2_, ...), custom_call_target="tpu_custom_call" | custom-call | tf_op jit(solution)/shard_map/hand_over/pallas_call | solution.py:524

commit v4 on v3

v4 whole, which is shorter than its diff:
```python
import math

import jax
import jax.numpy as jnp
from jax import lax
from jax.experimental import pallas as pl
from jax.experimental.pallas import tpu as pltpu
from jax.sharding import Mesh
from jax.sharding import PartitionSpec as P

FEAT = ("feat_0", "feat_1")
DP = ("dp_0", "dp_1")

UNITS = 8
UNIT = 4 * 128
BLOCK = UNITS * UNIT
SIZES = (2, 2, 2, 1, 1)
NC = len(SIZES)
CHUNKS = tuple((sum(SIZES[:c]), SIZES[c]) for c in range(NC))
DIRECT_SUMS = ((0, NC - 1), (1, NC - 1))
DIRECT_RESIDUALS = ((0, NC - 1),)
BF16, F32 = jnp.bfloat16, jnp.float32


def dot(a, b):
    return lax.dot_general(a, b, (((1,), (0,)), ((), ())), preferred_element_type=F32)


def kernel(rows_total, group_total, *refs):
    feats, sources, targets, rest = refs[0], refs[1:8], refs[8:13], refs[13:]
    body(rows_total, group_total, feats, sources, targets, *rest)


def body(rows_total, group_total, feats, sources, targets,
           labels, groups, coef_ref, coef_mom_ref, group_ref, group_mom_ref, scale_ref,
           coef_out, coef_mom_out, group_out, group_mom_out, energy_ref,
           X, ST, XO, OHT, W, PL, R1, R2, RG, CS, CG, ACC, GS, GC, GR, DB, DC, EN, LL, DIFF,
           POS, MOM, IV, STEP, HALF, NEW, WIDE,
           loc_sem, in_sem, out_sem, a_s, a_r, rs_s, rs_r, g_s, g_r, c_s, c_r, h_s, h_r, q_s, q_r, d_s, d_r, e_s, e_r):
    x, core = lax.axis_index("dp_0"), lax.axis_index("dp_1")
    place = (lax.axis_index("feat_0"), lax.axis_index("feat_1"))
    classes = coef_ref.shape[0]

    def at(axis, step):
        return {FEAT[axis]: lax.rem(place[axis] + step, 4)}

    def feat_at(k):
        return {**at(0, k // 4), **at(1, k % 4)}

    def dp_at(k):
        return {"dp_0": lax.rem(x + k, 4)} if k else {"dp_1": 1 - core}

    def remote(src, dst, s, r, device):
        return pltpu.make_async_remote_copy(
            src_ref=src, dst_ref=dst, send_sem=s, recv_sem=r,
            device_id=device, device_id_type=pl.DeviceIdType.MESH)

    def a2a(t, c, k):
        me = place[t]
        unit, units = CHUNKS[c]
        chunk, half = units * UNIT, units * UNIT // 2

        def rows(step, part, count):
            first = (t * 4 + lax.rem(me + step, 4)) * BLOCK + unit * UNIT + part * half
            return feats.at[pl.ds(pl.multiple_of(first, UNIT // 2), count)]

        def to(r, part, count):
            return X.at[t, r, pl.ds(unit * UNIT + part * half, count)]

        def staged(part):
            return ST.at[t, part, pl.ds(unit * UNIT // 2, half)]

        sems = (a_s.at[0], a_r.at[t, c, 1 if k in (2, 3) else 0])
        if k == 0:
            return remote(rows(1, 0, chunk), to(3, 0, chunk), *sems, at(t, 1))
        if k == 1:
            return remote(rows(3, 0, chunk), to(1, 0, chunk), *sems, at(t, 3))
        if k == 2:
            return remote(rows(2, 0, half), staged(0), *sems, at(t, 1))
        if k == 3:
            return remote(rows(2, 1, half), staged(1), *sems, at(t, 3))
        if k == 4:
            return remote(staged(0), to(2, 0, half), *sems, at(t, 1))
        return remote(staged(1), to(2, 1, half), *sems, at(t, 3))

    def scatter(e, t, c, k):
        axis = 1 - t
        p = place[axis]
        step = 1 if k % 2 == 0 else 3
        if k < 2 and (e, c) in DIRECT_SUMS:
            step = 2
        owner = lax.rem(p + (2 if k < 2 else step), 4)
        part = pl.ds((0, 1, 1, 0, 0, 1)[k] * 32, 32)
        units = pl.ds(*CHUNKS[c])
        dst = R1.at[e, t, k, units] if k < 2 else R2.at[e, t, k % 2, units, part]
        return remote(PL.at[e, t, units, owner, part], dst, rs_s.at[e], rs_r.at[e, t, c, 0 if k < 2 else 1], at(axis, step))

    def gather(e, t, c, k):
        axis = 1 - t
        p = place[axis]
        step = 2 if k == 4 else 1 if k % 2 == 0 else 3
        units = pl.ds(*CHUNKS[c])
        ref = RG.at[e, t, units, p]
        if k in (2, 3):
            ref = RG.at[e, t, units, lax.rem(p + 4 - step, 4), pl.ds((k - 2) * 32, 32)]
        return remote(ref, ref, g_s.at[e], g_r.at[e, t, c, 0 if k < 2 else 1], at(axis, step))

    def both(device, other):
        return {**device, "dp_1": 1 - core} if other else device

    def weights(e, t, r, other):
        if e == 0:
            return remote(CS.at[0, other], CG.at[0, t, 3 - r, other], c_s.at[0], c_r.at[0, t], at(t, r))
        half = CS.at[e, core]
        return remote(half, CG.at[e, t, 3 - r, core], c_s.at[e], c_r.at[e, t], both(at(t, r), other))

    def weights_across(e):
        half = CS.at[e, core]
        return remote(half, half, h_s.at[e, 0], h_r.at[e, 0], dp_at(0))

    def gradients_across(e):
        return remote(GS.at[e, 1 - core], GC.at[e], h_s.at[e, 1], h_r.at[e, 1], dp_at(0))

    def gradients(e, t, r):
        return remote(GS.at[e, core, t, r], GR.at[e, t, r - 1], q_s.at[e], q_r.at[e, t], at(t, r))

    def chips(e, k):
        return remote(DB.at[e, x], DB.at[e, x], d_s.at[e], d_r.at[e], dp_at(k))

    def totals_across(e):
        return remote(DC.at[e, core], DC.at[e, core], h_s.at[e, 2], h_r.at[e, 2], dp_at(0))

    def energies(k, other):
        mine = EN.at[core * 16 + place[0] * 4 + place[1]]
        return remote(mine, mine, e_s.at[0], e_r.at[0], both(feat_at(k), other))

    def bytes_of(ref, sem):
        pltpu.make_async_copy(ref, ref, sem).wait()

    def own(t):
        first = (t * 4 + place[t]) * BLOCK
        return pltpu.make_async_copy(feats.at[pl.ds(pl.multiple_of(first, BLOCK), BLOCK)], X.at[t, 0], loc_sem.at[t])

    def fetch(i):
        local = (labels, groups, coef_ref, coef_mom_ref, group_ref, group_mom_ref, scale_ref)[i]
        return pltpu.make_async_copy(sources[i], local, in_sem.at[i])

    def store(i):
        local = (coef_out, coef_mom_out, group_out, group_mom_out, energy_ref)[i]
        return pltpu.make_async_copy(local, targets[i], out_sem.at[i])

    lane = lax.broadcasted_iota(jnp.int32, (32, 128), 1)
    low = lane < 64

    barrier = pltpu.get_barrier_semaphore()

    @jax.named_call
    def enter():
        peers = [at(axis, k) for axis in range(2) for k in range(1, 4)] + [dp_at(k) for k in range(4)]
        for peer in peers:
            pl.semaphore_signal(barrier, inc=1, device_id=peer, device_id_type=pl.DeviceIdType.MESH)
        for i in (2, 4, 3, 5, 6, 0, 1):
            fetch(i).start()

    @jax.named_call
    def met():
        pl.semaphore_wait(barrier, 10)

    def pack(square):
        WIDE[:, 0:64] = square
        wide = WIDE[...]
        return jnp.concatenate([wide, pltpu.roll(wide, 96, 1)], axis=0).T[:32]

    def unpack(both):
        tall = jnp.concatenate([both, jnp.zeros((96, 128), F32)], axis=0).T
        return jnp.where(lax.broadcasted_iota(jnp.int32, (64, 128), 1) < 32, tall[:64], pltpu.roll(tall[64:], 32, 1))[:, :64]

    def keep(ref, top, bottom):
        ref[0] = top[0:48]
        ref[1, 0:16], ref[1, 16:48] = top[48:64], bottom

    def kept(first, second):
        return jnp.concatenate([first, second[0:16]], axis=0), second[16:48]

    @jax.named_call
    def prepare():
        WIDE[...] = jnp.zeros_like(WIDE)
        DIFF[...] = jnp.zeros_like(DIFF)
        ACC[...] = jnp.zeros_like(ACC)
        for i in (2, 4, 3, 5, 6):
            fetch(i).wait()
        keep(POS, coef_ref[...], pack(group_ref[...]))
        CS[0] = POS[...].astype(BF16)
        keep(MOM, coef_mom_ref[...], pack(group_mom_ref[...]))
        keep(IV, jnp.ones((64, 128), F32), pack(jnp.broadcast_to(jnp.exp(-2.0 * scale_ref[...]), (64, 64))))
        row = lax.broadcasted_iota(jnp.int32, (48, 128), 0)
        small, large = 4.0 / math.sqrt(rows_total), 4.0 * math.sqrt(group_total / rows_total)
        STEP[0] = jnp.full((48, 128), small, F32)
        STEP[1] = jnp.where(row < classes - 48, small, large)

    @jax.named_call
    def send_weights(e):
        if e:
            weights_across(e).start()
        for t in range(2):
            for r in (2, 1, 3):
                for other in range(2):
                    weights(e, t, r, other).start()

    @jax.named_call
    def gather_weights(e):
        if e:
            weights_across(e).wait_recv()
        for t in range(2):
            bytes_of(CG.at[e, t], c_r.at[e, t])
            packed = []
            for r in range(4):
                first, second = (CS[e, 0], CS[e, 1]) if r == 0 else (CG[e, t, r - 1, 0], CG[e, t, r - 1, 1])
                W[t, 0:48, r * 128:(r + 1) * 128] = first
                W[t, 48:64, r * 128:(r + 1) * 128] = second[0:16]
                packed.append(second[16:48].astype(F32))
            for i in range(2):
                a, b = packed[2 * i], packed[2 * i + 1]
                lanes = pl.ds(512 + i * 128, 128)
                W[t, 0:32, lanes] = jnp.where(low, a, pltpu.roll(b, 64, 1)).astype(BF16)
                W[t, 32:64, lanes] = jnp.where(low, pltpu.roll(a, 64, 1), b).astype(BF16)

    @jax.named_call
    def onehots():
        ids = lax.broadcasted_iota(jnp.int32, (64, 128), 0)
        for t in range(2):
            def onehot(u, _):
                for h in range(4):
                    group = groups[pl.ds(((t * 4 + place[t]) * UNITS + u) * 4 + h, 1), :]
                    for r in range(4):
                        other = lax.rem(place[t] + r, 4)
                        owner = other * 4 + place[1] if t == 0 else place[0] * 4 + other
                        hit = ids + owner * 64 == group
                        XO[t, u, 512 + r * 64:512 + (r + 1) * 64, h * 128:(h + 1) * 128] = \
                            jnp.where(hit, 1.0, 0.0).astype(BF16)
                OHT[t, u] = XO[t, u, 512:768].T
                return 0
            lax.fori_loop(0, UNITS, onehot, 0)

    @jax.named_call
    def send_features(c):
        for k in (2, 3, 0, 1):
            for t in range(2):
                a2a(t, c, k).start()

    @jax.named_call
    def pass_features(c):
        for t in range(2):
            bytes_of(X.at[t, 0, pl.ds(0, CHUNKS[c][1] * UNIT)], a_r.at[t, c, 1])
            a2a(t, c, 4).start()
            a2a(t, c, 5).start()

    @jax.named_call
    def wait_features(c):
        for t in range(2):
            bytes_of(X.at[t, pl.ds(1, 3), pl.ds(0, CHUNKS[c][1] * UNIT)], a_r.at[t, c, 0])

    def units_of(c):
        return range(CHUNKS[c][0], sum(CHUNKS[c]))

    def rows_of(u):
        return slice(u * UNIT, (u + 1) * UNIT)

    @jax.named_call
    def turn(c):
        for t in range(2):
            for u in units_of(c):
                for r in range(4):
                    XO[t, u, r * 128:(r + 1) * 128] = X[t, r, rows_of(u), :].T

    @jax.named_call
    def logits(e, c):
        for t in range(2):
            for u in units_of(c):
                total = dot(W[t], XO[t, u])
                for o in range(4):
                    PL[e, t, u, o] = total[:, o * 128:(o + 1) * 128]
            for k in range(6 if (e, c) in DIRECT_SUMS else 4):
                scatter(e, t, c, k).start()

    @jax.named_call
    def add_passed(e, c):
        if (e, c) in DIRECT_SUMS:
            return
        for t in range(2):
            p = place[1 - t]
            bytes_of(R1.at[e, t, :, pl.ds(*CHUNKS[c])], rs_r.at[e, t, c, 0])
            for k in range(2):
                owner = lax.rem(p + (1 if k == 0 else 3), 4)
                part = pl.ds(k * 32, 32)
                for u in units_of(c):
                    PL[e, t, u, owner, part] = PL[e, t, u, owner, part] + R1[e, t, k, u]
            for k in (4, 5):
                scatter(e, t, c, k).start()

    @jax.named_call
    def softmax(e, c):
        for t in range(2):
            p = place[1 - t]
            bytes_of(R2.at[e, t, :, pl.ds(*CHUNKS[c])], rs_r.at[e, t, c, 1])
            if (e, c) in DIRECT_SUMS:
                bytes_of(R1.at[e, t, :, pl.ds(*CHUNKS[c])], rs_r.at[e, t, c, 0])
            for u in units_of(c):
                value = PL[e, t, u, p] + R2[e, t, 0, u] + R2[e, t, 1, u]
                if (e, c) in DIRECT_SUMS:
                    value = value + jnp.concatenate([R1[e, t, 0, u], R1[e, t, 1, u]], axis=0)
                label = labels[pl.ds(((t * 4 + place[t]) * UNITS + u) * 4 + p, 1), :]
                shifted = value - jnp.max(value, axis=0, keepdims=True)
                scaled = jnp.exp(shifted)
                normalizer = jnp.sum(scaled, axis=0, keepdims=True)
                hit = lax.broadcasted_iota(jnp.int32, value.shape, 0) == label
                probability = scaled * (1.0 / normalizer)
                RG[e, t, u, p] = (jnp.where(hit, 1.0, 0.0) - probability).astype(BF16)
                loglik = jnp.sum(jnp.where(hit, shifted, 0.0), axis=0, keepdims=True) - jnp.log(normalizer)
                if e == 0:
                    LL[t, u] = jnp.broadcast_to(loglik, (8, 128))
                else:
                    DIFF[...] = DIFF[...] + (LL[t, u] - loglik)
            for k in (4, 0, 1) if (e, c) in DIRECT_RESIDUALS else (0, 1):
                gather(e, t, c, k).start()

    def accumulate(e, t, c, steps):
        owners = [lax.rem(place[1 - t] + step, 4) for step in steps]
        runs = [(u, o) for u in units_of(c) for o in owners]
        res = jnp.concatenate([RG[e, t, u, o] for u, o in runs], axis=1)
        rows = [pl.ds(pl.multiple_of(u * UNIT + o * 128, 128), 128) for u, o in runs]
        for r in (0, 2):
            two = jnp.concatenate(
                [jnp.concatenate([X[t, r, row, :], X[t, r + 1, row, :]], axis=1) for row in rows], axis=0)
            ACC[t, :, r * 128:(r + 2) * 128] += dot(res, two)
        onehot = jnp.concatenate([OHT[t, u, pl.ds(pl.multiple_of(o * 128, 128), 128)] for u, o in runs], axis=0)
        ACC[t, :, 512:768] += dot(res, onehot)

    @jax.named_call
    def pass_residual(e, c):
        for t in range(2):
            bytes_of(RG.at[e, t, pl.ds(*CHUNKS[c]), pl.ds(0, 2)], g_r.at[e, t, c, 0])
            if (e, c) in DIRECT_RESIDUALS:
                continue
            gather(e, t, c, 2).start()
            gather(e, t, c, 3).start()

    @jax.named_call
    def near_gradient(e, c):
        for t in range(2):
            accumulate(e, t, c, (0, 1, 3))

    @jax.named_call
    def gradient(e, c):
        for t in range(2):
            bytes_of(RG.at[e, t, pl.ds(*CHUNKS[c]), 0], g_r.at[e, t, c, 1])
            accumulate(e, t, c, (2,))

    @jax.named_call
    def core_sum(e):
        for t in range(2):
            for r in range(4):
                tile = 512 + (r // 2) * 128
                top, bottom = ACC[t, 0:32, tile:tile + 128], ACC[t, 32:64, tile:tile + 128]
                lanes = slice(r * 128, (r + 1) * 128)
                GS[e, 0, t, r] = ACC[t, 0:48, lanes]
                GS[e, 1, t, r, 0:16] = ACC[t, 48:64, lanes]
                if r % 2 == 0:
                    GS[e, 1, t, r, 16:48] = jnp.where(low, top, pltpu.roll(bottom, 64, 1))
                else:
                    GS[e, 1, t, r, 16:48] = jnp.where(low, pltpu.roll(top, 64, 1), bottom)
        gradients_across(e).start()
        gradients_across(e).wait_recv()
        for r in (2, 1, 3, 0):
            for t in range(2):
                GS[e, core, t, r] = GS[e, core, t, r] + GC[e, t, r]
                if r:
                    gradients(e, t, r).start()

    @jax.named_call
    def ring_sum(e):
        total = GS[e, core, 0, 0] + GS[e, core, 1, 0]
        for t in range(2):
            bytes_of(GR.at[e, t], q_r.at[e, t])
            for r in range(3):
                total = total + GR[e, t, r]
        DB[e, x, 0:48] = total
        DB[e, x, 48:56] = DIFF[...]
        for k in (2, 1, 3):
            chips(e, k).start()

    @jax.named_call
    def chip_sum(e):
        bytes_of(DB.at[e, pl.ds(0, 3)], d_r.at[e])
        return ((DB[e, 0] + DB[e, 1]) + DB[e, 2]) + DB[e, 3]

    def shared(e):
        totals_across(e).wait_recv()
        return kept(DC[e, 0, 0:48], DC[e, 1, 0:48])

    @jax.named_call
    def left(e):
        if e == 0:
            bytes_of(X, a_s.at[0])
        most = pl.ds(0, UNITS * 3 // 4)
        bytes_of(PL.at[e, :, most], rs_s.at[e])
        bytes_of(RG.at[e, :, most], g_s.at[e])
        bytes_of(CG.at[e], c_s.at[e])
        bytes_of(GR.at[e], q_s.at[e])
        bytes_of(DB.at[e, pl.ds(0, 3)], d_s.at[e])
        if e:
            weights_across(e).wait_send()
        gradients_across(e).wait_send()
        totals_across(e).wait_send()

    enter()
    prepare()
    met()
    send_weights(0)
    send_features(0)
    own(0).start()
    own(1).start()
    fetch(0).wait()
    fetch(1).wait()
    onehots()
    gather_weights(0)
    own(0).wait()
    own(1).wait()

    def arrived(c):
        wait_features(c)
        turn(c)
        logits(0, c)

    for s in range(NC + 5):
        for lag, stage in ((-1, send_features), (0, pass_features), (1, arrived), (2, add_passed), (3, softmax),
                           (4, pass_residual), (4, near_gradient), (5, gradient)):
            if 0 <= s - lag < NC:
                stage(*((s - lag,) if lag < 2 else (0, s - lag)))

    core_sum(0)
    ring_sum(0)
    grad = chip_sum(0)[0:48]
    step, pos = STEP[core], POS[core]
    half = MOM[core] + 0.5 * step * (grad - pos * IV[core])
    new = pos + step * half
    CS[1, core] = new.astype(BF16)
    send_weights(1)
    HALF[...] = half
    NEW[...] = new
    DC[0, core, 48:56] = jnp.zeros((8, 128), F32)
    DC[0, core, 0:48] = new
    totals_across(0).start()
    ACC[...] = jnp.zeros_like(ACC)

    coef_out[...], group = shared(0)
    group_out[...] = unpack(group)
    store(0).start()
    store(2).start()
    gather_weights(1)
    left(0)

    for stage in (logits, add_passed, softmax, pass_residual, near_gradient, gradient):
        for c in range(NC):
            stage(1, c)

    core_sum(1)
    ring_sum(1)
    total = chip_sum(1)

    @jax.named_call
    def finish():
        half, new, pos, old = HALF[...], NEW[...], POS[core], MOM[core]
        mom = half + 0.5 * STEP[core] * (total[0:48] - new * IV[core])
        state = 0.5 * ((new * new - pos * pos) * IV[core] + (mom * mom - old * old))
        EN[core * 16 + place[0] * 4 + place[1]] = total[48:56] + jnp.sum(state, axis=0, keepdims=True)
        for k in (15, 10, 11, 14, 5, 6, 7, 9, 13, 2, 8, 1, 3, 4, 12, 0):
            for other in range(2):
                if k or other:
                    energies(k, other).start()
        DC[1, core, 48:56] = jnp.zeros((8, 128), F32)
        DC[1, core, 0:48] = mom
        totals_across(1).start()
        coef_mom_out[...], group = shared(1)
        group_mom_out[...] = unpack(group)
        store(1).start()
        store(3).start()
    finish()
    left(1)
    for i in range(4):
        store(i).wait()

    @jax.named_call
    def total_energy():
        bytes_of(EN.at[pl.ds(0, 31)], e_r.at[0])
        terms = EN[0]
        for i in range(1, 32):
            terms = terms + EN[i]
        energy_ref[...] = jnp.broadcast_to(jnp.sum(terms, axis=1, keepdims=True), (8, 128))
        store(4).start()
        bytes_of(EN.at[pl.ds(0, 31)], e_s.at[0])
        store(4).wait()
    total_energy()


def hand_over(*refs):
    for source, target in zip(refs[:5], refs[5:]):
        target[...] = source[0:1, 0:1] if target.shape == (1, 1) else source[...]


def per_device(
    features, labels, groups, coefficients, coef_momentum, group_effects, group_momentum, log_scale
):
    rows = labels.shape[0]
    classes = coefficients.shape[1]
    rows_total = rows * lax.axis_size(DP)
    group_total = group_effects.shape[0] * lax.axis_size(FEAT)
    vmem = pl.BlockSpec(memory_space=pltpu.VMEM)
    dma = pltpu.SemaphoreType.DMA
    shapes = [(64, 128), (64, 128), (64, 64), (64, 64)]
    results = pl.pallas_call(
        lambda *refs: kernel(rows_total, group_total, *refs),
        out_shape=[jax.ShapeDtypeStruct(s, F32) for s in shapes + [(8, 128)]],
        in_specs=[pl.BlockSpec(memory_space=pl.ANY)] * 8,
        out_specs=[pl.BlockSpec(memory_space=pl.ANY)] * 5,
        scratch_shapes=[
            pltpu.VMEM((rows // 128, 128), jnp.int32), pltpu.VMEM((rows // 128, 128), jnp.int32),
            pltpu.VMEM((64, 128), F32), pltpu.VMEM((64, 128), F32),
            pltpu.VMEM((64, 64), F32), pltpu.VMEM((64, 64), F32), pltpu.VMEM((1, 64), F32),
            pltpu.VMEM((64, 128), F32), pltpu.VMEM((64, 128), F32),
            pltpu.VMEM((64, 64), F32), pltpu.VMEM((64, 64), F32), pltpu.VMEM((8, 128), F32),
            pltpu.VMEM((2, 4, BLOCK, 128), BF16),
            pltpu.VMEM((2, 2, BLOCK // 2, 128), BF16),
            pltpu.VMEM((2, UNITS, 768, UNIT), BF16),
            pltpu.VMEM((2, UNITS, UNIT, 256), BF16),
            pltpu.VMEM((2, 64, 768), BF16),
            pltpu.VMEM((2, 2, UNITS, 4, 64, 128), F32),
            pltpu.VMEM((2, 2, 2, UNITS, 32, 128), F32),
            pltpu.VMEM((2, 2, 2, UNITS, 64, 128), F32),
            pltpu.VMEM((2, 2, UNITS, 4, 64, 128), BF16),
            pltpu.VMEM((2, 2, 48, 128), BF16),
            pltpu.VMEM((2, 2, 3, 2, 48, 128), BF16),
            pltpu.VMEM((2, 64, 768), F32),
            pltpu.VMEM((2, 2, 2, 4, 48, 128), F32),
            pltpu.VMEM((2, 2, 4, 48, 128), F32),
            pltpu.VMEM((2, 2, 3, 48, 128), F32),
            pltpu.VMEM((2, 4, 56, 128), F32),
            pltpu.VMEM((2, 2, 56, 128), F32),
            pltpu.VMEM((32, 8, 128), F32),
            pltpu.VMEM((2, UNITS, 8, 128), F32),
            pltpu.VMEM((8, 128), F32),
            pltpu.VMEM((2, 48, 128), F32), pltpu.VMEM((2, 48, 128), F32), pltpu.VMEM((2, 48, 128), F32),
            pltpu.VMEM((2, 48, 128), F32), pltpu.VMEM((48, 128), F32), pltpu.VMEM((48, 128), F32),
            pltpu.VMEM((64, 128), F32),
            dma((2,)), dma((7,)), dma((5,)),
            dma((1,)), dma((2, NC, 2)),
            dma((2,)), dma((2, 2, NC, 2)),
            dma((2,)), dma((2, 2, NC, 2)),
            dma((2,)), dma((2, 2)),
            dma((2, 3)), dma((2, 3)),
            dma((2,)), dma((2, 2)),
            dma((2,)), dma((2,)),
            dma((1,)), dma((1,)),
        ],
        compiler_params=pltpu.CompilerParams(
            collective_id=0, has_side_effects=True, vmem_limit_bytes=58 * 2**20),
        name="leapfrog",
    )(features, labels.reshape(-1, 128), groups.reshape(-1, 128), coefficients.T, coef_momentum.T,
      group_effects, group_momentum, log_scale.reshape(1, -1))
    coef, coef_mom, group, group_mom, energy = pl.pallas_call(
        hand_over,
        out_shape=[jax.ShapeDtypeStruct(s, F32) for s in shapes + [(1, 1)]],
        in_specs=[vmem] * 5,
        out_specs=[vmem] * 5,
        name="hand_over",
    )(*results)
    return (coef.T, coef_mom.T, group, group_mom, energy[0, 0])


def solution(mesh):
    torus = Mesh(mesh.devices.reshape(4, 2, 4, 4), ("dp_0", "dp_1", "feat_0", "feat_1"))
    in_specs = (
        P(DP, FEAT),
        P(DP),
        P(DP),
        P(FEAT, None),
        P(FEAT, None),
        P(FEAT, None),
        P(FEAT, None),
        P(),
    )
    out_specs = (P(FEAT, None), P(FEAT, None), P(FEAT, None), P(FEAT, None), P())
    return jax.shard_map(
        per_device, mesh=torus, in_specs=in_specs, out_specs=out_specs, check_vma=False
    )
```

time: 127 us -> 124 us (0.976)
  Pallas kernels: 126 us -> 123 us
    pallas_call x1, Pallas kernels: 125 us -> 121 us  [per_device(): pl.pallas_call(lambda *refs: kernel(rows_total, group_total, *refs), out_...]
where the time goes in v4:
time: 124 us; the launch traced here: 123 us
  Pallas kernels  123 us (99%)
    pallas_call x1, Pallas kernels, per_device(): pl.pallas_call(lambda *refs: kernel(rows_total, group_total, *refs), out_...  121 us

profile of v4, /device:TPU:1, one launch (start us, length us, event | category | flops | bytes accessed | tf_op | source)
XLA Modules:
  0.0 123.5 jit_solution(13926441398540742260)
XLA Ops:
  0.6 121.3 %leapfrog.1 = (f32[64,128]{1,0:T(8,128)}, f32[64,128]{1,0:T(8,128)}, f32[64,64]{1,0:T(8,128)}, f32[64,64]{1,0:T(8,128)}, f32[8,128]{1,0:T(8,128)}) custom-call(bf16[32768,128]{1,0:T(8,128)(2,1)} %refs_0_.1, s32[256,128]{1,0:T(8,128)} %bitcast.8, s32[256,128]{1,0:T(8,128)} %bitcast.9, f32[64,128]{1,0:T(8,128)} %bitcast.10, f32[64,128]{1,0:T(8,128)} %bitcast.11, ...), custom_call_target="tpu_custom_call" | custom-call | tf_op jit(solution)/shard_map/leapfrog/pallas_call | solution.py:521
  122.0 1.5 %hand_over.1 = (f32[64,128]{1,0:T(8,128)}, f32[64,128]{1,0:T(8,128)}, f32[64,64]{1,0:T(8,128)}, f32[64,64]{1,0:T(8,128)}, f32[1,1]{1,0:T(1,128)}) custom-call(f32[64,128]{1,0:T(8,128)} %get-tuple-element.15.refs_0_, f32[64,128]{1,0:T(8,128)} %get-tuple-element.16.refs_1_, f32[64,64]{1,0:T(8,128)} %get-tuple-element.17.refs_2_, ...), custom_call_target="tpu_custom_call" | custom-call | tf_op jit(solution)/shard_map/hand_over/pallas_call | solution.py:570
